TPU v7x, 32 devices: a whole 2x2x4 slice. The times are simulated.
32 devices in a mesh: groups: 1, row: 16 (over z, y, x), col: 2 (over core).
Axes of the slice: x: 2, y: 2, z: 4, core: 2. Of those that a mesh axis runs over, the one named last changes fastest.
Arguments:
- wave_now: float32 [2, 2048, 4096], P('groups', 'row', 'col'), may hold values from -6 to 6
- wave_before: float32 [2, 2048, 4096], P('groups', 'row', 'col'), may hold values from -6 to 6
- fault_slip: float32 [2048, 4096], P(('groups', 'row'), 'col'), may hold values from 0 to 2
- region_ids: int32 [128, 256], P(('groups', 'row'), 'col'), may hold values from 0 to 7
- mode_history: bfloat16 [16, 2, 4096, 2048], P('groups', None, ('row', 'col')), may hold values from -6 to 6
- wave_kernel: bfloat16 [16, 4096, 2048], P(None, ('row', 'col')), may hold values from -1.5 to 1.5
- static_friction: float32 [8], replicated, may hold values from 0.55 to 0.75
- dynamic_friction: float32 [8], replicated, may hold values from 0.2 to 0.45
- weakening_slip: float32 [8], replicated, may hold values from 0.3 to 3
- normal_stress: float32 [8], replicated, may hold values from 2 to 5
- initial_stress: float32 [8], replicated, may hold values from -1.5 to 1.5
Outputs:
- final_wave: float32 [2, 2048, 4096], P('groups', 'row', 'col')
- final_slip: float32 [2048, 4096], P(('groups', 'row'), 'col')
- fault_traction: float32 [2048, 4096], P(('groups', 'row'), 'col')
All inputs are finite; a program needn't handle non-finite values.
Results may differ from a plain program's by a relative error of at most 0.0003.
Values sent between devices are 32-bit elements; how exact they have to be, the bound alone decides.
No kernel may reach another device: no remote copies, remote signals or barrier semaphores. Data moves between devices by JAX's collectives and lax.ppermute only.
A program may use at most 128 MiB of HBM per device.

v0:
```python
import math

import jax
import jax.numpy as jnp
from jax import lax
from jax.sharding import PartitionSpec as P

SUBSTEPS = 2
BLOCK_CELLS = 16


damping = 0.5
courant = 0.3
highest = lax.Precision.HIGHEST


def with_halo(cells, sides, width):
    for axis, dim in sides:
        count = lax.axis_size(axis)
        head = lax.slice_in_dim(cells, 0, width, axis=dim)
        tail = lax.slice_in_dim(cells, cells.shape[dim] - width, cells.shape[dim], axis=dim)
        cells = jnp.concatenate(
            [
                lax.ppermute(tail, axis, [(i, (i + 1) % count) for i in range(count)]),
                cells,
                lax.ppermute(head, axis, [((i + 1) % count, i) for i in range(count)]),
            ],
            axis=dim,
        )
    return cells


def phase_table(first_count, second_count, modulus, sign):
    first = lax.broadcasted_iota(jnp.int32, (first_count, second_count), 0)
    second = lax.broadcasted_iota(jnp.int32, (first_count, second_count), 1)
    product = first * second % modulus
    angle = sign * 2.0 * math.pi / modulus * product.astype(jnp.float32)
    return (jnp.cos(angle), jnp.sin(angle))


def contract(form, left, right):
    return jnp.einsum(form, left, right, precision=highest, preferred_element_type=jnp.float32)


def complex_contract(form, left, right):
    real_part = contract(form, left[0], right[0]) - contract(form, left[1], right[1])
    imag_part = contract(form, left[0], right[1]) + contract(form, left[1], right[0])
    return (real_part, imag_part)


def complex_scale(pair, factor):
    return (pair[0] * factor[0] - pair[1] * factor[1], pair[0] * factor[1] + pair[1] * factor[0])


def forward_along_y(values):
    row_count, width = values.shape
    outer = 64
    inner = width // outer
    shaped = values.reshape(row_count, outer, inner)
    first_table = phase_table(outer, outer, outer, -1.0)
    sectioned = (
        contract("kn,rnm->rkm", first_table[0], shaped),
        contract("kn,rnm->rkm", first_table[1], shaped),
    )
    twiddle = phase_table(outer, inner, width, -1.0)
    sectioned = complex_scale(sectioned, (twiddle[0][None], twiddle[1][None]))
    second_table = phase_table(inner, inner, inner, -1.0)
    result = complex_contract("rkm,mq->qkr", sectioned, second_table)
    stacked = jnp.stack([result[0].reshape(width, row_count), result[1].reshape(width, row_count)])
    return stacked / math.sqrt(width)


def forward_along_x(pieces):
    blocks, span, block_rows = (pieces.shape[1], pieces.shape[2], pieces.shape[3])
    length = blocks * block_rows
    first_table = phase_table(blocks, blocks, blocks, -1.0)
    sectioned = complex_contract("ks,sji->kji", first_table, (pieces[0], pieces[1]))
    twiddle = phase_table(blocks, block_rows, length, -1.0)
    sectioned = complex_scale(sectioned, (twiddle[0][:, None, :], twiddle[1][:, None, :]))
    second_table = phase_table(block_rows, block_rows, block_rows, -1.0)
    result = complex_contract("kji,iq->jqk", sectioned, second_table)
    stacked = jnp.stack([result[0].reshape(span, length), result[1].reshape(span, length)])
    return stacked / math.sqrt(length)


def inverse_along_x(spectrum, blocks):
    span, length = (spectrum.shape[1], spectrum.shape[2])
    block_rows = length // blocks
    shaped = spectrum.reshape(2, span, block_rows, blocks)
    first_table = phase_table(block_rows, block_rows, block_rows, 1.0)
    sectioned = complex_contract("am,jmn->jan", first_table, (shaped[0], shaped[1]))
    twiddle = phase_table(block_rows, blocks, length, 1.0)
    sectioned = complex_scale(sectioned, (twiddle[0][None], twiddle[1][None]))
    second_table = phase_table(blocks, blocks, blocks, 1.0)
    result = complex_contract("jan,nb->bja", sectioned, second_table)
    stacked = jnp.stack(
        [result[0].reshape(blocks, span * block_rows), result[1].reshape(blocks, span * block_rows)]
    )
    return stacked / math.sqrt(length)


def inverse_along_y(spectrum):
    width, row_count = (spectrum.shape[1], spectrum.shape[2])
    outer = 64
    inner = width // outer
    shaped = spectrum.reshape(2, outer, inner, row_count)
    first_table = phase_table(outer, outer, outer, 1.0)
    sectioned = complex_contract("am,mnr->anr", first_table, (shaped[0], shaped[1]))
    twiddle = phase_table(outer, inner, width, 1.0)
    sectioned = complex_scale(sectioned, (twiddle[0][:, :, None], twiddle[1][:, :, None]))
    second_table = phase_table(inner, inner, inner, 1.0)
    real_part = contract("anr,nb->rba", sectioned[0], second_table[0]) - contract(
        "anr,nb->rba", sectioned[1], second_table[1]
    )
    return real_part.reshape(row_count, width) / math.sqrt(width)


def shards(
    wave_now,
    wave_before,
    fault_slip,
    region_ids,
    mode_history,
    wave_kernel,
    static_friction,
    dynamic_friction,
    weakening_slip,
    normal_stress,
    initial_stress,
):
    tile_rows, tile_cols = (wave_now.shape[1], wave_now.shape[2])
    row_count = lax.axis_size("row")
    col_count = lax.axis_size("col")
    col_index = lax.axis_index("col")
    blocks = row_count * col_count
    full_width = tile_cols * col_count
    span = full_width // blocks
    block_rows = region_ids.shape[0]
    block_cols = region_ids.shape[1]
    cell_ids = jnp.broadcast_to(
        region_ids[:, None, :, None], (block_rows, BLOCK_CELLS, block_cols, BLOCK_CELLS)
    ).reshape(tile_rows, tile_cols)
    region_mask = (
        cell_ids[None] == jnp.arange(static_friction.shape[0], dtype=jnp.int32)[:, None, None]
    )

    def lookup(table):
        return jnp.sum(jnp.where(region_mask, table[:, None, None], 0.0), axis=0)

    static_level = lookup(static_friction)
    dynamic_level = lookup(dynamic_friction)
    weakening = lookup(weakening_slip)
    normal_load = lookup(normal_stress)
    prestress = lookup(initial_stress)
    horizon = mode_history.shape[0]
    current = wave_now
    previous = wave_before
    slip = fault_slip
    traction = jnp.zeros_like(fault_slip)
    recent = []
    for substep in range(SUBSTEPS):
        slip_rate = current[0] - previous[0]
        padded = with_halo(current, (("row", 1), ("col", 2)), 1)
        whole_rows = lax.all_gather(slip_rate, "col", axis=1, tiled=True)
        columns = forward_along_y(whole_rows)
        own_part = lax.dynamic_index_in_dim(
            columns.reshape(2, row_count, col_count, -1), col_index, 2, keepdims=False
        )
        spread = lax.all_to_all(own_part, "row", split_axis=1, concat_axis=1, tiled=True)
        spectrum = forward_along_x(spread.reshape(2, row_count, span, tile_rows))
        recent.insert(0, spectrum)
        fresh = len(recent)
        wave_load = jnp.einsum(
            "hjk,hcjk->cjk",
            wave_kernel[fresh:],
            mode_history[: horizon - fresh],
            preferred_element_type=jnp.float32,
        )
        for offset in range(fresh):
            wave_load = wave_load + wave_kernel[offset].astype(jnp.float32)[None] * recent[offset]
        back_part = inverse_along_x(wave_load, row_count)
        returned = lax.all_to_all(back_part, "row", split_axis=1, concat_axis=1, tiled=True)
        joined = lax.all_gather(returned[:, :, None, :], "col", axis=2, tiled=True)
        whole_field = inverse_along_y(joined.reshape(2, full_width, tile_rows))
        far_field = lax.dynamic_slice_in_dim(whole_field, col_index * tile_cols, tile_cols, 1)
        trial_stress = prestress + far_field - damping * slip_rate
        strength = normal_load * (
            static_level - (static_level - dynamic_level) * jnp.minimum(slip / weakening, 1.0)
        )
        traction = jnp.clip(trial_stress, -strength, strength)
        slip = slip + jnp.abs(slip_rate)
        laplacian = (
            padded[:, 2:, 1:-1]
            + padded[:, :-2, 1:-1]
            + padded[:, 1:-1, 2:]
            + padded[:, 1:-1, :-2]
            - 4.0 * current
        )
        upper_cells = jnp.concatenate([current[1:], jnp.zeros_like(current[:1])], 0)
        lower_cells = jnp.concatenate([(current[0] + traction)[None], current[:-1]], 0)
        following = (
            2.0 * current
            - previous
            + courant * (laplacian + upper_cells + lower_cells - 2.0 * current)
        )
        previous = current
        current = following
    return (current, slip, traction)


def solution(mesh):
    return jax.shard_map(
        shards,
        mesh=mesh,
        in_specs=(
            P("groups", "row", "col"),
            P("groups", "row", "col"),
            P(("groups", "row"), "col"),
            P(("groups", "row"), "col"),
            P("groups", None, ("row", "col"), None),
            P(None, ("row", "col"), None),
            P(),
            P(),
            P(),
            P(),
            P(),
        ),
        out_specs=(
            P("groups", "row", "col"),
            P(("groups", "row"), "col"),
            P(("groups", "row"), "col"),
        ),
        check_vma=False,
    )
```

profile of v0, /device:TPU:0, one launch (start us, length us, event | category | flops | bytes accessed | tf_op | source)
XLA Modules:
  0.0 564.3 jit_solution(7440012928844400356)
XLA Ops:
  7.2 2.7 bitcast_subtract_fusion.1
  10.0 13.3 %all-gather.7.cloned.1.call-done = f32[128,4096]{1,0:T(8,128)} async-done(((f32[128,2048]{1,0:T(8,128)}), f32[128,4096]{1,0:T(8,128)}) %all-gather.7.cloned.1.call-update) | async-done | bytes 2097168 | tf_op jit(solution)/shard_map/all_gather | solution.py:164
  25.3 3.4 fusion.74
  28.6 4.5 fusion.24
  33.1 3.1 fusion.64
  36.2 3.4 fusion.66
  39.6 3.1 subtract_bitcast_fusion.1
  42.8 3.2 add_bitcast_fusion.1
  48.5 3.5 stack.27
  54.5 4.0 stack.26
  58.5 4.3 fusion.34
  62.9 2.9 copy.778
  65.8 6.8 %all-to-all-start = ((f32[2,16,16384]{2,0,1:T(2,128)}), f32[2,16,16384]{2,0,1:T(2,128)}, u32[]{:S(2)}, u32[]{:S(2)}) async-start(f32[2,16,16384]{2,0,1:T(2,128)} %bitcast.290), calls=%async_computation | async-start | bytes 4194304 | tf_op jit(solution)/shard_map/all_to_all | solution.py:169
  75.5 11.0 %bitcast_convert_fusion = f32[128,2048,15]{1,0,2:T(8,128)} fusion(bf16[16,128,2048]{2,1,0:T(8,128)(2,1)} %param.16), kind=kLoop, calls=%fused_computation.8 | loop fusion | flops 3932160 | bytes 23592960
  86.5 13.7 %multiply_reduce_fusion = f32[128,2048,2]{1,0,2:T(8,128)} fusion(f32[128,2048,15]{1,0,2:T(8,128)} %bitcast_convert_fusion, bf16[16,2,128,2048]{3,2,1,0:T(8,128)(2,1)} %param.15), kind=kLoop, calls=%fused_computation | loop fusion | flops 23068672 | bytes 33554432
  102.4 13.6 %all-to-all-done = f32[2,16,16384]{2,0,1:T(2,128)} async-done(((f32[2,16,16384]{2,0,1:T(2,128)}), f32[2,16,16384]{2,0,1:T(2,128)}, u32[]{:S(2)}, u32[]{:S(2)}) %all-to-all-start) | async-done | bytes 2097184 | tf_op jit(solution)/shard_map/all_to_all | solution.py:169
  116.0 4.4 fusion.537
  150.7 58.6 %all_to_all.20 = f32[2,16,16384]{2,0,1:T(2,128)} all-to-all(f32[2,16,16384]{2,0,1:T(2,128)S(1)} %copy.494), channel_id=1, replica_groups=mesh['groups'=1,'row'=16,'col'=2] {'row'}, dimensions={1} | all-to-all | bytes 4194304 | tf_op jit(solution)/shard_map/all_to_all | solution.py:182
  210.9 2.6 collective-permute-start
  213.5 5.4 broadcast_in_dim.79
  218.9 7.9 %eq.44 = s32[128,2048]{1,0:T(8,128)S(1)} reshape(s32[8,16,128,16]{3,2,1,0:T(8,128)} %broadcast_in_dim.79) | data formatting | bytes 2097152 | tf_op jit(solution)/shard_map/eq | solution.py:144
  228.4 7.2 %select_reduce_fusion.2 = (f32[128,2048]{1,0:T(8,128)}, f32[128,2048]{1,0:T(8,128)}, f32[128,2048]{1,0:T(8,128)}, f32[128,2048]{1,0:T(8,128)}, f32[128,2048]{1,0:T(8,128)}) fusion(f32[8]{0:T(128)S(1)} %copy-done.24, s32[128,2048]{1,0:T(8,128)S(1)} %eq.44, f32[8]{0:T(128)S(1)} %copy-done.25, f32[8]{0:T(128)S(1)} %copy-done.26, f32[8]{0:T(128)S(1)} %copy-done.27, ...), kind=kLoop, calls=%fused_computation.4 | loop fusion | flops 21757952 | bytes 6291616 | tf_op jit(solution)/shard_map/reduce_sum | solution.py:148
  237.1 7.7 %fusion.530 = (f32[1,16,32768]{2,0,1:T(1,128)S(1)}, f32[1,16,32768]{2,0,1:T(1,128)S(1)}) fusion(f32[2,16,32768]{2,0,1:T(2,128)} %all-gather.11.cloned.1.call-done), kind=kLoop, calls=%fused_computation.608 | loop fusion | bytes 8388608 | tf_op jit(solution)/shard_map/slice | solution.py:108
  244.8 3.1 fusion.56
  248.0 3.1 fusion.58
  251.1 3.3 fusion.80
  254.5 4.2 multiply_subtract_fusion.1
  258.6 3.1 fusion.30
  261.7 3.5 multiply_bitcast_fusion.1
  270.2 4.2 fusion.109
  274.5 4.4 fusion.17
  281.0 12.1 %all-gather.9.cloned.1.call-done = f32[128,4096]{1,0:T(8,128)} async-done(((f32[128,2048]{1,0:T(8,128)}), f32[128,4096]{1,0:T(8,128)}) %all-gather.9.cloned.1.call-update) | async-done | bytes 2097168 | tf_op jit(solution)/shard_map/all_gather | solution.py:164
  293.0 2.9 copy.513
  296.0 5.1 fusion.54
  301.0 4.5 fusion.22
  305.5 3.1 fusion.44
  308.6 3.3 fusion.46
  312.0 4.5 subtract_bitcast_fusion
  316.5 3.2 add_bitcast_fusion
  319.7 2.6 copy.523
  322.2 3.5 stack.32
  325.7 4.2 copy.520
  329.9 3.7 stack.31
  333.6 5.0 fusion.35
  338.6 3.0 copy.777
  341.6 6.8 %all-to-all-start.2 = ((f32[2,16,16384]{2,0,1:T(2,128)}), f32[2,16,16384]{2,0,1:T(2,128)}, u32[]{:S(2)}, u32[]{:S(2)}) async-start(f32[2,16,16384]{2,0,1:T(2,128)} %bitcast.315), calls=%async_computation.2 | async-start | bytes 4194304 | tf_op jit(solution)/shard_map/all_to_all | solution.py:169
  351.0 10.1 %bitcast_convert_fusion.1 = f32[128,2048,14]{1,0,2:T(8,128)} fusion(bf16[16,128,2048]{2,1,0:T(8,128)(2,1)} %param.16), kind=kLoop, calls=%fused_computation.9 | loop fusion | flops 3670016 | bytes 22020096
  361.1 13.3 %multiply_reduce_fusion.1 = f32[128,2048,2]{1,0,2:T(8,128)} fusion(f32[128,2048,14]{1,0,2:T(8,128)} %bitcast_convert_fusion.1, bf16[16,2,128,2048]{3,2,1,0:T(8,128)(2,1)} %param.15), kind=kLoop, calls=%fused_computation.1 | loop fusion | flops 21495808 | bytes 31457280
  374.4 3.3 copy.596
  377.7 14.0 %all-to-all-done.2 = f32[2,16,16384]{2,0,1:T(2,128)} async-done(((f32[2,16,16384]{2,0,1:T(2,128)}), f32[2,16,16384]{2,0,1:T(2,128)}, u32[]{:S(2)}, u32[]{:S(2)}) %all-to-all-start.2) | async-done | bytes 2097184 | tf_op jit(solution)/shard_map/all_to_all | solution.py:169
  391.7 4.4 fusion.533
  417.9 2.6 fusion.152
  443.8 58.5 %all_to_all.21 = f32[2,16,16384]{2,0,1:T(2,128)} all-to-all(f32[2,16,16384]{2,0,1:T(2,128)S(1)} %copy.554), channel_id=1, replica_groups=mesh['groups'=1,'row'=16,'col'=2] {'row'}, dimensions={1} | all-to-all | bytes 4194304 | tf_op jit(solution)/shard_map/all_to_all | solution.py:182
  506.3 3.4 fusion.531
  509.7 3.9 collective-permute-done.5
  514.9 7.7 %fusion.529 = (f32[1,16,32768]{2,0,1:T(1,128)S(1)}, f32[1,16,32768]{2,0,1:T(1,128)S(1)}) fusion(f32[2,16,32768]{2,0,1:T(2,128)} %all-gather.13.cloned.1.call-done), kind=kLoop, calls=%fused_computation.607 | loop fusion | bytes 8388608 | tf_op jit(solution)/shard_map/slice | solution.py:108
  522.7 3.1 fusion.36
  525.8 3.1 fusion.38
  529.0 3.3 fusion.90
  532.3 4.1 multiply_subtract_fusion
  536.4 3.1 fusion.26
  539.6 3.4 multiply_bitcast_fusion
  547.8 5.9 %fusion.108 = (f32[1,128,2048]{2,1,0:T(8,128)S(1)}, f32[128,2048]{1,0:T(8,128)}) fusion(f32[2,128,2048]{2,1,0:T(8,128)} %copy-done.1, f32[128,2048]{1,0:T(8,128)} %get-tuple-element.18, f32[128,2048]{1,0:T(8,128)} %get-tuple-element.13, f32[128,2048]{1,0:T(8,128)} %copy.644, f32[128,2048]{1,0:T(8,128)} %get-tuple-element.16, ...), kind=kLoop, calls=%fused_computation.161 | loop fusion | flops 3932160 | bytes 12582912 | tf_op jit(solution)/shard_map/broadcast_in_dim | solution.py:200
  553.7 3.8 fusion.8
  (168 shorter events, 111.5 us)
Async XLA Ops:
  7.2 16.2 %all-gather.7.cloned.1.call-start = ((), (), s32[]{:S(2)}) async-start(), calls=%async_computation.4 | async-start | bytes 3145728 | tf_op jit(solution)/shard_map/all_gather | solution.py:164
  54.5 4.0 copy-start.16
  65.8 50.1 %all-to-all-start = ((f32[2,16,16384]{2,0,1:T(2,128)}), f32[2,16,16384]{2,0,1:T(2,128)}, u32[]{:S(2)}, u32[]{:S(2)}) async-start(f32[2,16,16384]{2,0,1:T(2,128)} %bitcast.290), calls=%async_computation | async-start | bytes 4194304 | tf_op jit(solution)/shard_map/all_to_all | solution.py:169
  72.7 164.4 %all-gather.11.cloned.1.call-start = ((), (), s32[]{:S(2)}) async-start(), calls=%async_computation.6 | async-start | bytes 6291456 | tf_op jit(solution)/shard_map/all_gather | solution.py:183
  75.5 58.9 %copy-start.6 = (f32[128,2048]{0,1:T(8,128)}, f32[128,2048]{0,1:T(8,128)S(1)}, u32[]{:S(2)}) copy-start(f32[128,2048]{0,1:T(8,128)S(1)} %copy.483) | copy-start | bytes 3145732
  133.7 1.0 copy-start.8
  134.3 1.1 copy-start.10
  209.2 1.6 copy-start
  209.2 4.3 copy-start.23
  209.3 83.8 %all-gather.9.cloned.1.call-start = ((), (), s32[]{:S(2)}) async-start(), calls=%async_computation.5 | async-start | bytes 3145728 | tf_op jit(solution)/shard_map/all_gather | solution.py:164
  210.9 24.9 %collective-permute-start = (f32[2,1,2048]{2,0,1:T(2,128)S(1)}, f32[2,1,2048]{2,0,1:T(2,128)S(1)}, u32[]{:S(2)}, u32[]{:S(2)}) collective-permute-start(f32[2,1,2048]{2,0,1:T(2,128)S(1)} %copy.641), channel_id=1, source_target_pairs={{2,0},{4,2},{6,4},{8,6},{10,8},{12,10},{14,12},{16,14},{18,16},{20... | collective-permute-start | bytes 49160 | tf_op jit(solution)/shard_map/ppermute | solution.py:26
  213.5 22.3 %collective-permute-start.1 = (f32[2,1,2048]{2,0,1:T(2,128)S(1)}, f32[2,1,2048]{2,0,1:T(2,128)S(1)}, u32[]{:S(2)}, u32[]{:S(2)}) collective-permute-start(f32[2,1,2048]{2,0,1:T(2,128)S(1)} %copy.642), channel_id=1, source_target_pairs={{0,2},{2,4},{4,6},{6,8},{8,10},{10,12},{12,14},{14,16},{16,18},{18... | collective-permute-start | bytes 49160 | tf_op jit(solution)/shard_map/ppermute | solution.py:24
  226.8 1.5 copy-start.24
  226.8 1.5 copy-start.25
  226.8 1.5 copy-start.26
  226.8 1.5 copy-start.27
  226.9 1.5 copy-start.28
  236.6 37.8 %collective-permute-start.2 = (f32[2,130,1]{2,1,0:T(8,128)}, f32[2,130,1]{2,1,0:T(8,128)S(1)}, u32[]{:S(2)}, u32[]{:S(2)}) collective-permute-start(f32[2,130,1]{2,1,0:T(8,128)} %get-tuple-element.37), channel_id=1, source_target_pairs={{1,0},{0,1},{3,2},{2,3},{5,4},{4,5},{7,6},{6,7},{9,8},{8,9},{11,10... | collective-permute-start | bytes 3128 | tf_op jit(solution)/shard_map/ppermute | solution.py:26
  236.6 37.8 %collective-permute-start.3 = (f32[2,130,1]{2,1,0:T(8,128)}, f32[2,130,1]{2,1,0:T(8,128)}, u32[]{:S(2)}, u32[]{:S(2)}) collective-permute-start(f32[2,130,1]{2,1,0:T(8,128)} %get-tuple-element.38), channel_id=1, source_target_pairs={{0,1},{1,0},{2,3},{3,2},{4,5},{5,4},{6,7},{7,6},{8,9},{9,8},{10,11... | collective-permute-start | bytes 3128 | tf_op jit(solution)/shard_map/ppermute | solution.py:24
  266.5 3.6 copy-start.4
  270.1 4.3 copy-start.17
  270.1 4.3 copy-start.19
  270.1 4.3 copy-start.20
  274.5 4.4 copy-start.12
  278.9 2.0 copy-start.1
  296.0 5.1 copy-start.5
  341.6 50.2 %all-to-all-start.2 = ((f32[2,16,16384]{2,0,1:T(2,128)}), f32[2,16,16384]{2,0,1:T(2,128)}, u32[]{:S(2)}, u32[]{:S(2)}) async-start(f32[2,16,16384]{2,0,1:T(2,128)} %bitcast.315), calls=%async_computation.2 | async-start | bytes 4194304 | tf_op jit(solution)/shard_map/all_to_all | solution.py:169
  348.4 166.5 %all-gather.13.cloned.1.call-start = ((), (), s32[]{:S(2)}) async-start(), calls=%async_computation.7 | async-start | bytes 6291456 | tf_op jit(solution)/shard_map/all_gather | solution.py:183
  407.2 2.8 copy-start.15
  408.7 1.3 copy-start.7
  408.8 1.5 copy-start.9
  408.8 1.8 copy-start.11
  408.8 2.1 copy-start.18
  417.9 2.6 copy-start.13
  417.9 3.9 copy-start.14
  503.3 10.3 %copy-start.2 = (f32[2,128,2048]{2,1,0:T(8,128)S(1)}, f32[2,128,2048]{2,1,0:T(8,128)}, u32[]{:S(2)}) copy-start(f32[2,128,2048]{2,1,0:T(8,128)} %copy-done.1) | copy-start | bytes 6291460
  503.3 6.4 %collective-permute-start.4 = (f32[2,1,2048]{2,0,1:T(2,128)S(1)}, f32[2,1,2048]{2,0,1:T(2,128)S(1)}, u32[]{:S(2)}, u32[]{:S(2)}) collective-permute-start(f32[2,1,2048]{2,0,1:T(2,128)S(1)} %copy.507), channel_id=1, source_target_pairs={{2,0},{4,2},{6,4},{8,6},{10,8},{12,10},{14,12},{16,14},{18,16},{20... | collective-permute-start | bytes 49160 | tf_op jit(solution)/shard_map/ppermute | solution.py:26
  505.9 7.7 %collective-permute-start.5 = (f32[2,1,2048]{2,0,1:T(2,128)S(1)}, f32[2,1,2048]{2,0,1:T(2,128)S(1)}, u32[]{:S(2)}, u32[]{:S(2)}) collective-permute-start(f32[2,1,2048]{2,0,1:T(2,128)S(1)} %copy.509), channel_id=1, source_target_pairs={{0,2},{2,4},{4,6},{6,8},{8,10},{10,12},{12,14},{14,16},{16,18},{18... | collective-permute-start | bytes 49160 | tf_op jit(solution)/shard_map/ppermute | solution.py:24
  514.4 39.3 %collective-permute-start.6 = (f32[2,130,1]{2,1,0:T(8,128)}, f32[2,130,1]{2,1,0:T(8,128)S(1)}, u32[]{:S(2)}, u32[]{:S(2)}) collective-permute-start(f32[2,130,1]{2,1,0:T(8,128)} %get-tuple-element.35), channel_id=1, source_target_pairs={{1,0},{0,1},{3,2},{2,3},{5,4},{4,5},{7,6},{6,7},{9,8},{8,9},{11,10... | collective-permute-start | bytes 3128 | tf_op jit(solution)/shard_map/ppermute | solution.py:26
  514.4 39.3 %collective-permute-start.7 = (f32[2,130,1]{2,1,0:T(8,128)}, f32[2,130,1]{2,1,0:T(8,128)S(1)}, u32[]{:S(2)}, u32[]{:S(2)}) collective-permute-start(f32[2,130,1]{2,1,0:T(8,128)} %get-tuple-element.36), channel_id=1, source_target_pairs={{0,1},{1,0},{2,3},{3,2},{4,5},{5,4},{6,7},{7,6},{8,9},{9,8},{10,11... | collective-permute-start | bytes 3128 | tf_op jit(solution)/shard_map/ppermute | solution.py:24
  547.8 5.9 %copy-start.3 = (f32[2,128,2048]{2,1,0:T(8,128)S(1)}, f32[2,128,2048]{2,1,0:T(8,128)}, u32[]{:S(2)}) copy-start(f32[2,128,2048]{2,1,0:T(8,128)} %copy-done.1) | copy-start | bytes 6291460
  547.8 6.0 %copy-start.21 = (f32[1,128,2048]{2,1,0:T(8,128)S(1)}, f32[1,128,2048]{2,1,0:T(8,128)}, u32[]{:S(2)}) copy-start(f32[1,128,2048]{2,1,0:T(8,128)} %get-tuple-element.47) | copy-start | bytes 3145732
  547.8 6.0 %copy-start.22 = (f32[1,128,2048]{2,1,0:T(8,128)S(1)}, f32[1,128,2048]{2,1,0:T(8,128)}, u32[]{:S(2)}) copy-start(f32[1,128,2048]{2,1,0:T(8,128)} %get-tuple-element.48) | copy-start | bytes 3145732
Sparse Core Ops, SparseCore 0:
  10.0 13.2 all-gather.6
  209.4 12.0 all-gather.10
  281.1 11.9 all-gather.8
  502.4 12.0 all-gather.12
where the time goes:
time: 575 us; the launch traced here: 564 us
  matrix products  135 us (23%)
  local copies, waits for them, and re-layouts  125 us (22%)
  blocking collectives  117 us (20%)
  other arithmetic  94.6 us (16%)
  waiting for transfers between devices  56.9 us (10%)
  starting transfers between devices  20.5 us (4%)
  between operations  15.1 us (3%)
    dot_general x56, matrix products, contract(): jnp.einsum(form, left, right, precision=highest, preferred_element_type=j...  135 us
    all_to_all x2, blocking collectives, shards(): lax.all_to_all(back_part, 'row', split_axis=1, concat_axis=1, tiled=True)  117 us
    unnamed x4, other arithmetic  48.1 us
    all_to_all x2, waiting for transfers between devices, shards(): lax.all_to_all(own_part, 'row', split_axis=1, concat_axis=1, tiled=True)  27.6 us
    all_gather x2, waiting for transfers between devices, shards(): whole_rows = lax.all_gather(slip_rate, 'col', axis=1, tiled=True)  25.4 us
    slice x2, local copies, waits for them, and re-layouts, inverse_along_y(): shaped[0]  15.5 us
    another operation x4, local copies, waits for them, and re-layouts, forward_along_y(): jnp.stack([result[0].reshape(width, row_count), result[1].reshape(width,...  14.7 us
    all_to_all x2, starting transfers between devices, shards(): lax.all_to_all(own_part, 'row', split_axis=1, concat_axis=1, tiled=True)  13.7 us
  transfers between devices with their start and end apart: 14, of which 5 were waited for; matrix products, arithmetic and copies ran while one was open for 29% of the time, Pallas kernels for 0%

commit v1 on v0

v1 whole, which is shorter than its diff:
```python
import functools
import math

import jax
import jax.numpy as jnp
import numpy as np
from jax import lax
from jax.experimental import pallas as pl
from jax.experimental.pallas import tpu as pltpu
from jax.sharding import PartitionSpec as P

SUBSTEPS = 2
BLOCK_CELLS = 16
LANES = 128
SUB = 8

damping = 0.5
courant = 0.3
f32 = jnp.float32
bf16 = jnp.bfloat16


def add(a, b):
    if a is None:
        return b
    return a if b is None else a + b


def sub(a, b):
    if b is None:
        return a
    return -b if a is None else a - b


def scale(z, w):
    re, im = z
    c, s = w.real, w.imag
    if abs(s) < 1e-12:
        return (re, im) if c > 0 else (-re, None if im is None else -im)
    if abs(c) < 1e-12:
        if s > 0:
            return (None if im is None else -im, re)
        return (im, None if re is None else -re)
    if im is None:
        return (re * c, re * s)
    if re is None:
        return (im * -s, im * c)
    if abs(abs(c) - abs(s)) < 1e-12:
        a = abs(c)
        signs = (c > 0, s > 0)
        if signs == (True, True):
            return ((re - im) * a, (re + im) * a)
        if signs == (True, False):
            return ((re + im) * a, (im - re) * a)
        if signs == (False, True):
            return ((re + im) * -a, (re - im) * a)
        return ((im - re) * a, (re + im) * -a)
    return (re * c - im * s, re * s + im * c)


def cadd(a, b):
    return (add(a[0], b[0]), add(a[1], b[1]))


def csub(a, b):
    return (sub(a[0], b[0]), sub(a[1], b[1]))


def conj(a):
    return (a[0], None if a[1] is None else -a[1])


def root(k, n, sign):
    return complex(math.cos(2 * math.pi * k / n), sign * math.sin(2 * math.pi * k / n))


def fft_list(zs, sign):
    n = len(zs)
    if n == 1:
        return list(zs)
    even = fft_list(zs[0::2], sign)
    odd = fft_list(zs[1::2], sign)
    low, high = [], []
    for k in range(n // 2):
        t = scale(odd[k], root(k, n, sign))
        low.append(cadd(even[k], t))
        high.append(csub(even[k], t))
    return low + high


def rfft_list(xs):
    n = len(xs)
    if n == 1:
        return [(xs[0], None)]
    if n == 2:
        return [(xs[0] + xs[1], None), (xs[0] - xs[1], None)]
    even = rfft_list(xs[0::2])
    odd = rfft_list(xs[1::2])
    out = [None] * (n // 2 + 1)
    for k in range(n // 4 + 1):
        t = scale(odd[k], root(k, n, -1.0))
        out[k] = cadd(even[k], t)
        if n // 2 - k != k:
            out[n // 2 - k] = conj(csub(even[k], t))
    return out


def irfft_list(ps):
    n = 2 * (len(ps) - 1)
    if n == 2:
        return [ps[0][0] + ps[1][0], ps[0][0] - ps[1][0]]
    even, odd = [], []
    for k in range(n // 4 + 1):
        mirrored = conj(ps[n // 2 - k])
        even.append(cadd(ps[k], mirrored))
        odd.append(scale(csub(ps[k], mirrored), root(k, n, 1.0)))
    a, b = irfft_list(even), irfft_list(odd)
    return [v for pair in zip(a, b) for v in pair]


def halves(table):
    high = table.astype(np.float32).astype(bf16)
    low = (table - high.astype(np.float64)).astype(np.float32).astype(bf16)
    return jnp.asarray(high), jnp.asarray(low)


def complex_block(re, im):
    return np.block([[re, im], [-im, re]])


def make_tables(width, length, row_count, col_count):
    span = width // (row_count * col_count)
    n_count = span // SUB
    m_count = width // n_count
    rows = length // row_count
    m = np.arange(m_count)
    q = (np.arange(row_count)[:, None] * (col_count * SUB) + np.arange(SUB)[None, :]).reshape(-1)
    angle = 2 * np.pi * np.outer(m, q) / m_count
    forward_y = halves(complex_block(np.cos(angle), -np.sin(angle)))
    inverse_y = halves(complex_block(np.cos(angle.T), np.sin(angle.T)))
    i = np.arange(rows)
    angle = 2 * np.pi * np.outer(i, i) / rows
    forward_x = halves(complex_block(np.cos(angle), -np.sin(angle)))
    inverse_x = halves(complex_block(np.cos(angle), np.sin(angle)))
    k = np.arange(n_count)
    col = np.arange(col_count)[:, None, None]
    angle = 2 * np.pi * (k[:, None] * m[None, :] / width + col * SUB * m[None, None, :] / m_count)
    angle = angle + np.pi * col * k[:, None]
    norm = 1 / math.sqrt(width)
    turn_y = np.stack([np.cos(angle), np.sin(angle)], 2) * norm
    k = np.arange(row_count)
    angle = 2 * np.pi * np.outer(k, i) / length
    turn_x = np.stack([np.cos(angle), np.sin(angle)], 1) / math.sqrt(length)
    return dict(
        forward_y=forward_y,
        inverse_y=inverse_y,
        forward_x=forward_x,
        inverse_x=inverse_x,
        turn_y=jnp.asarray(turn_y, f32),
        turn_x=jnp.asarray(turn_x, f32),
    )


def split(z):
    high = z.astype(bf16)
    return high, (z - high.astype(f32)).astype(bf16)


def product(z, table_high, table_low):
    high, low = split(z)
    dot = functools.partial(jnp.dot, preferred_element_type=f32)
    return dot(high, table_high) + dot(low, table_high) + dot(high, table_low)


def group_of(count, rows):
    group = count
    while group > 1 and group * rows > 512:
        group //= 2
    return group


def lane_width(count):
    return min(LANES, count)


def forward_y_kernel(n_count, own, other, turn, table_high, table_low, out, work):
    rows = own.shape[0]
    m_count = turn.shape[2]
    lane = lane_width(m_count)
    half = n_count // 2

    def tile(t, carry):
        at = pl.ds(pl.multiple_of(t * SUB, SUB), SUB)
        for j in range(m_count // lane):
            xs = []
            for ref in (own, other):
                for n in range(half):
                    begin = n * m_count + j * lane
                    xs.append(ref[at, begin : begin + lane])
            spectrum = rfft_list(xs)
            for k in range(n_count):
                z = spectrum[k] if k <= half else conj(spectrum[n_count - k])
                c = turn[k, 0:1, j * lane : (j + 1) * lane]
                s = turn[k, 1:2, j * lane : (j + 1) * lane]
                if z[1] is None:
                    re, im = z[0] * c, z[0] * -s
                else:
                    re, im = z[0] * c + z[1] * s, z[1] * c - z[0] * s
                work[k, at, j * lane : (j + 1) * lane] = re
                work[k, at, m_count + j * lane : m_count + (j + 1) * lane] = im
        return carry

    lax.fori_loop(0, rows // SUB, tile, 0)
    group = group_of(n_count, rows)
    row_count = out.shape[0]
    q_count = row_count * SUB
    for g in range(0, n_count, group):
        z = work[g : g + group].reshape(group * rows, 2 * m_count)
        o = product(z, table_high[...], table_low[...])
        for k in range(group):
            for c in range(2):
                block = o[k * rows : (k + 1) * rows, c * q_count : (c + 1) * q_count]
                begin = (g + k) * SUB
                out[:, c, begin : begin + SUB, :] = block.T.reshape(row_count, SUB, rows)


def middle_kernel(
    last, data, turn, forward_high, forward_low, inverse_high, inverse_low, first_kernel, load, *rest
):
    if last:
        out, work = rest
    else:
        second_kernel, later_load, out, later_out, work = rest
    row_count, _, span, rows = data.shape

    def gather(t, carry):
        at = pl.ds(pl.multiple_of(t * SUB, SUB), SUB)
        zs = fft_list([(data[s, 0, at, :], data[s, 1, at, :]) for s in range(row_count)], -1.0)
        for k in range(row_count):
            c, s = turn[k, 0:1, :], turn[k, 1:2, :]
            work[k, at, :rows] = zs[k][0] * c + zs[k][1] * s
            work[k, at, rows:] = zs[k][1] * c - zs[k][0] * s
        return carry

    lax.fori_loop(0, span // SUB, gather, 0)
    group = group_of(row_count, span)
    for g in range(0, row_count, group):
        z = work[g : g + group].reshape(group * span, 2 * rows)
        spectrum = product(z, forward_high[...], forward_low[...]).reshape(group, span, 2 * rows)
        parts = (spectrum[:, :, :rows], spectrum[:, :, rows:])
        factor = first_kernel[g : g + group]
        loads = [load[c, g : g + group] + factor * parts[c] for c in range(2)]
        if not last:
            factor = second_kernel[g : g + group]
            for c in range(2):
                later_out[c, g : g + group] = later_load[c, g : g + group] + factor * parts[c]
        w = jnp.concatenate(loads, axis=2).reshape(group * span, 2 * rows)
        w = product(w, inverse_high[...], inverse_low[...])
        work[g : g + group] = w.reshape(group, span, 2 * rows)

    def scatter(t, carry):
        at = pl.ds(pl.multiple_of(t * SUB, SUB), SUB)
        zs = []
        for k in range(row_count):
            c, s = turn[k, 0:1, :], turn[k, 1:2, :]
            re, im = work[k, at, :rows], work[k, at, rows:]
            zs.append((re * c - im * s, im * c + re * s))
        zs = fft_list(zs, 1.0)
        for k in range(row_count):
            out[k, 0, at, :] = zs[k][0]
            out[k, 1, at, :] = zs[k][1]
        return carry

    lax.fori_loop(0, span // SUB, scatter, 0)


def inverse_y_kernel(n_count, data, turn, table_high, table_low, own, other, work):
    row_count, _, _, rows = data.shape
    m_count = turn.shape[2]
    lane = lane_width(m_count)
    half = n_count // 2
    q_count = row_count * SUB
    group = group_of(n_count, rows)
    for g in range(0, n_count, group):
        blocks = []
        for k in range(g, g + group):
            parts = [data[:, c, k * SUB : (k + 1) * SUB, :].reshape(q_count, rows).T for c in range(2)]
            blocks.append(jnp.concatenate(parts, axis=1))
        z = jnp.concatenate(blocks, axis=0)
        o = product(z, table_high[...], table_low[...])
        work[g : g + group] = o.reshape(group, rows, 2 * m_count)

    def tile(t, carry):
        at = pl.ds(pl.multiple_of(t * SUB, SUB), SUB)
        for j in range(m_count // lane):
            ys = []
            for k in range(n_count):
                c = turn[k, 0:1, j * lane : (j + 1) * lane]
                s = turn[k, 1:2, j * lane : (j + 1) * lane]
                re = work[k, at, j * lane : (j + 1) * lane]
                im = work[k, at, m_count + j * lane : m_count + (j + 1) * lane]
                ys.append((re * c - im * s, im * c + re * s))
            ps = [(ys[0][0], None)]
            for k in range(1, half):
                both = cadd(ys[k], conj(ys[n_count - k]))
                ps.append((both[0] * 0.5, both[1] * 0.5))
            ps.append((ys[half][0], None))
            xs = irfft_list(ps)
            for n in range(half):
                begin = n * m_count + j * lane
                own[at, begin : begin + lane] = xs[n]
                other[at, begin : begin + lane] = xs[half + n]
        return carry

    lax.fori_loop(0, rows // SUB, tile, 0)


def load_kernel(kernel, history, loads, later_loads, first, second, sums, turned):
    horizon, block, length = kernel.shape
    step = pl.program_id(0)
    lane = lane_width(length)
    at = pl.ds(pl.multiple_of(step * block, block), block)

    def chunk(j, carry):
        cols = pl.ds(pl.multiple_of(j * lane, lane), lane)
        totals = [jnp.zeros((block, lane), f32) for _ in range(4)]
        factors = [kernel[h, :, cols].astype(f32) for h in range(horizon)]
        for h in range(horizon - 1):
            for c in range(2):
                past = history[h, c, :, cols].astype(f32)
                totals[c] = totals[c] + factors[h + 1] * past
                if h + 2 < horizon:
                    totals[2 + c] = totals[2 + c] + factors[h + 2] * past
        for a, total in enumerate((*totals, factors[0], factors[1])):
            sums[a, j, at, :] = total
        return carry

    lax.fori_loop(0, length // lane, chunk, 0)

    @pl.when(step == pl.num_programs(0) - 1)
    def _():
        span = sums.shape[2]
        n_count = span // SUB
        row_count, _, rows = first.shape

        def reorder(a, target):
            for j in range(length // lane):
                pieces = [sums[a, j, pl.ds(k, SUB, stride=n_count), :] for k in range(n_count)]
                turned[j * lane : (j + 1) * lane, :span] = jnp.concatenate(pieces, axis=0).T
            for k in range(row_count):
                target[k] = turned[pl.ds(k, rows, stride=row_count), :][:, :span].T

        reorder(0, loads.at[0])
        reorder(1, loads.at[1])
        reorder(2, later_loads.at[0])
        reorder(3, later_loads.at[1])
        reorder(4, first)
        reorder(5, second)


def stencil_kernel(current, previous, slip, cells, above, below, beside, base, strength, following, grown):
    rows, cols = slip.shape
    lane = beside.shape[2] // 2
    row_index = lax.broadcasted_iota(jnp.int32, (rows, cols), 0)
    col_index = lax.broadcasted_iota(jnp.int32, (rows, cols), 1)
    for layer in range(2):
        here = current[layer]
        up = pltpu.roll(here, 1, 0)
        up = jnp.where(row_index == 0, above[layer, SUB - 1 : SUB, :], up)
        down = pltpu.roll(here, rows - 1, 0)
        down = jnp.where(row_index == rows - 1, below[layer, 0:1, :], down)
        left = pltpu.roll(here, 1, 1)
        left = jnp.where(col_index == 0, beside[layer, :, 2 * lane - 1 : 2 * lane], left)
        right = pltpu.roll(here, cols - 1, 1)
        right = jnp.where(col_index == cols - 1, beside[layer, :, 0:1], right)
        flat = up + down + left + right - 4.0 * here
        if layer == 0:
            across = current[1] + here - 2.0 * here
        else:
            across = current[0] - 2.0 * here
        following[layer] = 2.0 * here - previous[layer] + courant * (flat + across)
    count = cells.shape[1]
    for r in range(count):
        at = slice(r * BLOCK_CELLS, (r + 1) * BLOCK_CELLS)
        rate = current[0, at, :] - previous[0, at, :]
        old = slip[at, :]
        base[at, :] = cells[3, r : r + 1, :] - damping * rate
        weak = jnp.minimum(old * cells[2, r : r + 1, :], 1.0)
        strength[at, :] = cells[0, r : r + 1, :] - cells[1, r : r + 1, :] * weak
        grown[at, :] = old + jnp.abs(rate)


def traction_kernel(own, other, base, strength, current, partial, following, result):
    limit = strength[...]
    traction = jnp.clip(base[...] + (own[...] + other[...]), -limit, limit)
    updated = partial[0] + courant * traction
    following[0] = updated
    result[...] = updated - current[0]


def last_traction_kernel(own, other, base, strength, partial, following, result):
    limit = strength[...]
    traction = jnp.clip(base[...] + (own[...] + other[...]), -limit, limit)
    result[...] = traction
    following[0] = partial[0] + courant * traction


def vmem():
    return pl.BlockSpec(memory_space=pltpu.VMEM)


def call(kernel, inputs, outputs, scratch=(), flops=0, name=None):
    size = sum(int(np.prod(v.shape)) * v.dtype.itemsize for v in (*inputs, *outputs))
    return pl.pallas_call(
        kernel,
        in_specs=[vmem()] * len(inputs),
        out_specs=[vmem()] * len(outputs),
        out_shape=list(outputs),
        scratch_shapes=list(scratch),
        cost_estimate=pl.CostEstimate(flops=flops, transcendentals=0, bytes_accessed=size),
        name=name,
    )(*inputs)


def shards(
    wave_now,
    wave_before,
    fault_slip,
    region_ids,
    mode_history,
    wave_kernel,
    static_friction,
    dynamic_friction,
    weakening_slip,
    normal_stress,
    initial_stress,
):
    rows, cols = wave_now.shape[1], wave_now.shape[2]
    row_count = lax.axis_size("row")
    col_count = lax.axis_size("col")
    assert col_count == 2 and SUBSTEPS == 2
    width, length = cols * col_count, rows * row_count
    span = width // (row_count * col_count)
    n_count = span // SUB
    m_count = width // n_count
    horizon = mode_history.shape[0]
    tables = make_tables(width, length, row_count, col_count)
    turn_y = lax.dynamic_index_in_dim(tables["turn_y"], lax.axis_index("col"), 0, keepdims=False)
    half_shape = jax.ShapeDtypeStruct((row_count, 2, span, rows), f32)
    tile_shape = jax.ShapeDtypeStruct((rows, cols), f32)
    load_shape = jax.ShapeDtypeStruct((2, row_count, span, rows), f32)
    factor_shape = jax.ShapeDtypeStruct((row_count, span, rows), f32)

    def swap(value):
        return lax.ppermute(value, "col", [(0, 1), (1, 0)])

    def regroup(value):
        return lax.all_to_all(value, "row", split_axis=0, concat_axis=0, tiled=True)

    chosen = region_ids[None] == jnp.arange(static_friction.shape[0], dtype=jnp.int32)[:, None, None]

    def lookup(table):
        return jnp.sum(jnp.where(chosen, table[:, None, None], 0.0), axis=0)

    normal_load = lookup(normal_stress)
    static_level = lookup(static_friction)
    blocks = jnp.stack(
        [
            normal_load * static_level,
            normal_load * (static_level - lookup(dynamic_friction)),
            1.0 / lookup(weakening_slip),
            lookup(initial_stress),
        ]
    )
    spread = np.repeat(np.eye(region_ids.shape[1], dtype=np.float32), BLOCK_CELLS, axis=1)
    cells = jnp.einsum("abc,cd->abd", blocks, spread, precision=lax.Precision.HIGHEST)

    block = 16
    past = jax.ShapeDtypeStruct
    loads, later_loads, first, second = pl.pallas_call(
        load_kernel,
        grid=(span // block,),
        in_specs=[
            pl.BlockSpec((horizon, block, length), lambda b: (0, b, 0)),
            pl.BlockSpec((horizon - 1, 2, block, length), lambda b: (0, 0, b, 0)),
        ],
        out_specs=[vmem()] * 4,
        out_shape=[load_shape, load_shape, factor_shape, factor_shape],
        scratch_shapes=[
            pltpu.VMEM((6, length // lane_width(length), span, lane_width(length)), f32),
            pltpu.VMEM((length, max(span, LANES)), f32),
        ],
        cost_estimate=pl.CostEstimate(
            flops=20 * horizon * span * length, transcendentals=0, bytes_accessed=6 * horizon * span * length
        ),
        name="past_loads",
    )(wave_kernel, mode_history)

    def forward(rate):
        work = pltpu.VMEM((n_count, rows, 2 * m_count), f32)
        inputs = (rate, swap(rate), turn_y, *tables["forward_y"])
        (part,) = call(
            functools.partial(forward_y_kernel, n_count), inputs, [half_shape], [work], 10**9, "forward_y"
        )
        return regroup(part)

    def middle(last, data, *more):
        work = pltpu.VMEM((row_count, span, 2 * rows), f32)
        outputs = [half_shape] if last else [half_shape, load_shape]
        inputs = (data, tables["turn_x"], *tables["forward_x"], *tables["inverse_x"], *more)
        return call(functools.partial(middle_kernel, last), inputs, outputs, [work], 10**9, "middle")

    def inverse(data):
        work = pltpu.VMEM((n_count, rows, 2 * m_count), f32)
        own, other = call(
            functools.partial(inverse_y_kernel, n_count),
            (data, turn_y, *tables["inverse_y"]),
            [tile_shape, tile_shape],
            [work],
            10**9,
            "inverse_y",
        )
        return own, swap(other)

    def stencil(current, previous, slip):
        ring = [(i, (i + 1) % row_count) for i in range(row_count)]
        above = lax.ppermute(current[:, rows - SUB :], "row", ring)
        below = lax.ppermute(current[:, :SUB], "row", [(b, a) for a, b in ring])
        edge = lane_width(cols)
        beside = swap(jnp.concatenate([current[:, :, :edge], current[:, :, cols - edge :]], axis=2))
        inputs = (current, previous, slip, cells, above, below, beside)
        outputs = [tile_shape, tile_shape, jax.ShapeDtypeStruct(current.shape, f32), tile_shape]
        return call(stencil_kernel, inputs, outputs, (), 5 * 10**8, "stencil")

    def traction_step(kernel, *inputs):
        step = 32 if rows % 32 == 0 else rows
        layer = pl.BlockSpec((1, step, cols), lambda i: (0, i, 0))
        tile = pl.BlockSpec((step, cols), lambda i: (i, 0))
        partial = inputs[-1]
        specs = [layer if v.ndim == 3 else tile for v in inputs]
        return pl.pallas_call(
            kernel,
            grid=(rows // step,),
            in_specs=specs,
            out_specs=[layer, tile],
            out_shape=[jax.ShapeDtypeStruct(partial.shape, f32), tile_shape],
            input_output_aliases={len(inputs) - 1: 0},
            name="traction",
        )(*inputs)

    data = forward(wave_now[0] - wave_before[0])
    base, strength, partial, slip = stencil(wave_now, wave_before, fault_slip)
    back, later_loads = middle(False, data, first, loads, second, later_loads)
    own, other = inverse(regroup(back))
    current, rate = traction_step(traction_kernel, own, other, base, strength, wave_now, partial)

    data = forward(rate)
    base, strength, partial, slip = stencil(current, wave_now, slip)
    (back,) = middle(True, data, first, later_loads)
    own, other = inverse(regroup(back))
    current, traction = traction_step(last_traction_kernel, own, other, base, strength, partial)
    return (current, slip, traction)


def solution(mesh):
    return jax.shard_map(
        shards,
        mesh=mesh,
        in_specs=(
            P("groups", "row", "col"),
            P("groups", "row", "col"),
            P(("groups", "row"), "col"),
            P(("groups", "row"), "col"),
            P("groups", None, ("row", "col"), None),
            P(None, ("row", "col"), None),
            P(),
            P(),
            P(),
            P(),
            P(),
        ),
        out_specs=(
            P("groups", "row", "col"),
            P(("groups", "row"), "col"),
            P(("groups", "row"), "col"),
        ),
        check_vma=False,
    )
```

time: 575 us -> 316 us (0.55); the launches traced: 564 us -> 315 us
  matrix products: 135 us -> 1.38 us
  local copies, waits for them, and re-layouts: 125 us -> 14 us
  other arithmetic: 94.6 us -> 2.52 us
  Pallas kernels: 0 us -> 84.7 us
  between operations: 15.1 us -> 0.81 us
  waiting for transfers between devices: 56.9 us -> 68.3 us
  starting transfers between devices: 20.5 us -> 31.7 us
  blocking collectives: 117 us -> 111 us
    dot_general x56 -> x1, matrix products: 135 us -> 1.38 us  [shards(): jnp.einsum('abc,cd->abd', blocks, spread, precision=lax.Precision.HIGHEST)]
    pallas_call x0 -> x11, Pallas kernels: none -> 84.7 us  [the longest x8 55 us: call(): pl.pallas_call(kernel, in_specs=[vmem()] * len(inputs), out_specs=[vmem()...]
    unnamed x4 -> x0, other arithmetic: 48.1 us -> none
    all_to_all x2, waiting for transfers between devices: 27.6 us -> 60.3 us  [regroup(): return lax.all_to_all(value, 'row', split_axis=0, concat_axis=0, tiled=True)]
    slice x12 -> x4, local copies, waits for them, and re-layouts: 31.7 us -> 4.61 us  [the longest x2 2.63 us: stencil(): below = lax.ppermute(current[:, :SUB], 'row', [(b, a) for a, b in ring])]
    all_gather x4 -> x0, waiting for transfers between devices: 25.4 us -> none  [the longest x2 25.4 us: shards(): whole_rows = lax.all_gather(slip_rate, 'col', axis=1, tiled=True)]
    another operation x8 -> x0, local copies, waits for them, and re-layouts: 19.9 us -> none  [the longest x4 14.7 us: forward_along_y(): jnp.stack([result[0].reshape(width, row_count), result[1].reshape(width,...]
    squeeze x6 -> x1, local copies, waits for them, and re-layouts: 11.9 us -> 0.61 us  [shards(): lax.dynamic_index_in_dim(tables['turn_y'], lax.axis_index('col'), 0, keep...]
  transfers between devices with their start and end apart: 14 -> 12, of which waited for: 5 -> 5; matrix products, arithmetic and copies ran while one was open for 29% -> 2% of each run, Pallas kernels for 0% -> 13%
where the time goes in v1:
time: 316 us; the launch traced here: 315 us
  blocking collectives  111 us (35%)
  Pallas kernels  84.7 us (27%)
  waiting for transfers between devices  68.3 us (22%)
  starting transfers between devices  31.7 us (10%)
  local copies, waits for them, and re-layouts  14 us (4%)
    all_to_all x2, blocking collectives, regroup(): return lax.all_to_all(value, 'row', split_axis=0, concat_axis=0, tiled=True)  111 us
    all_to_all x2, waiting for transfers between devices, regroup(): return lax.all_to_all(value, 'row', split_axis=0, concat_axis=0, tiled=True)  60.3 us
    pallas_call x8, Pallas kernels, call(): pl.pallas_call(kernel, in_specs=[vmem()] * len(inputs), out_specs=[vmem()...  55 us
    pallas_call x1, Pallas kernels, shards(): pl.pallas_call(load_kernel, grid=(span // block,), in_specs=[pl.BlockSpec...  20.7 us
    all_to_all x2, starting transfers between devices, regroup(): return lax.all_to_all(value, 'row', split_axis=0, concat_axis=0, tiled=True)  18.4 us
    ppermute x2, starting transfers between devices, stencil(): below = lax.ppermute(current[:, :SUB], 'row', [(b, a) for a, b in ring])  8.99 us
    pallas_call x2, Pallas kernels, traction_step(): pl.pallas_call(kernel, grid=(rows // step,), in_specs=specs, out_specs=[l...  8.97 us
    unnamed x38, local copies, waits for them, and re-layouts  8.75 us
  transfers between devices with their start and end apart: 12, of which 5 were waited for; matrix products, arithmetic and copies ran while one was open for 2% of the time, Pallas kernels for 13%

profile of v1, /device:TPU:0, one launch (start us, length us, event | category | flops | bytes accessed | tf_op | source)
XLA Modules:
  0.0 314.7 jit_solution(7227587016994188405)
XLA Ops:
  0.6 0.0 copy-start.14
  0.6 1.7 subtract_bitcast_fusion.own
  2.3 0.0 copy-start.1
  2.3 0.6 collective-permute-start
  2.9 0.0 copy-done.14
  2.9 0.6 dynamic-slice_bitcast_fusion.turn
  3.5 1.7 collective-permute-done.other
  5.2 0.0 copy-done.1
  5.2 1.0 copy-done.5
  6.2 5.9 %forward_y.2 = f32[16,2,128,128]{3,2,1,0:T(8,128)} custom-call(f32[128,2048]{1,0:T(8,128)} %copy-done.1, f32[128,2048]{1,0:T(8,128)} %copy-done.5, f32[16,2,256]{2,1,0:T(2,128)} %dynamic-slice_bitcast_fusion.turn, bf16[512,256]{1,0:T(8,128)(2,1)} %constant.36.clone.table_high, bf16[512,256]{1,0:T(8,128)(2,1)} %constant.37.clone.table_low), custom_call_target="tpu_custom_call" | custom-call | flops 1000000000 | bytes 4751360 | tf_op jit(solution)/shard_map/forward_y/pallas_call | solution.py:414
  12.1 8.2 %all-to-all-start = ((f32[16,2,128,128]{3,2,1,0:T(8,128)}), f32[16,2,128,128]{3,2,1,0:T(8,128)S(1)}, u32[]{:S(2)}, u32[]{:S(2)}) async-start(f32[16,2,128,128]{3,2,1,0:T(8,128)} %forward_y.2), calls=%async_computation | async-start | bytes 4194304 | tf_op jit(solution)/shard_map/all_to_all | solution.py:458
  20.3 20.7 %past_loads.1 = (f32[2,16,128,128]{3,2,1,0:T(8,128)}, f32[2,16,128,128]{3,2,1,0:T(8,128)}, f32[16,128,128]{2,1,0:T(8,128)}, f32[16,128,128]{2,1,0:T(8,128)}) custom-call(bf16[16,128,2048]{2,1,0:T(8,128)(2,1)} %kernel.1, bf16[16,2,128,2048]{3,2,1,0:T(8,128)(2,1)} %history.1), custom_call_target="tpu_custom_call" | custom-call | flops 83886080 | bytes 25165824 | tf_op jit(solution)/shard_map/past_loads/pallas_call | solution.py:480
  41.0 22.5 %all-to-all-done.data = f32[16,2,128,128]{3,2,1,0:T(8,128)S(1)} async-done(((f32[16,2,128,128]{3,2,1,0:T(8,128)}), f32[16,2,128,128]{3,2,1,0:T(8,128)S(1)}, u32[]{:S(2)}, u32[]{:S(2)}) %all-to-all-start) | async-done | bytes 2097184 | tf_op jit(solution)/shard_map/all_to_all | solution.py:458
  63.6 1.3 copy-done
  64.9 9.5 %middle.2 = (f32[16,2,128,128]{3,2,1,0:T(8,128)}, f32[2,16,128,128]{3,2,1,0:T(8,128)}) custom-call(f32[16,2,128,128]{3,2,1,0:T(8,128)} %copy-done, f32[16,2,128]{2,1,0:T(2,128)} %constant.45.clone.turn, bf16[256,256]{1,0:T(8,128)(2,1)} %constant.40.clone.forward_high, bf16[256,256]{1,0:T(8,128)(2,1)} %constant.41.clone.forward_low, ...), custom_call_target="tpu_custom_call" | custom-call | flops 1000000000 | bytes 13123584 | tf_op jit(solution)/shard_map/middle/pallas_call | solution.py:414
  74.4 10.2 %all-to-all-start.1 = ((f32[16,2,128,128]{3,2,1,0:T(8,128)}), f32[16,2,128,128]{3,2,1,0:T(8,128)S(1)}, u32[]{:S(2)}, u32[]{:S(2)}) async-start(f32[16,2,128,128]{3,2,1,0:T(8,128)} %get-tuple-element.29), calls=%async_computation.1 | async-start | bytes 4194304 | tf_op jit(solution)/shard_map/all_to_all | solution.py:458
  84.6 1.6 fusion.6
  86.2 1.9 collective-permute-start.2
  88.2 0.0 copy-start.3
  88.2 3.9 %collective-permute-start.3 = (f32[2,8,2048]{2,1,0:T(8,128)S(1)}, f32[2,8,2048]{2,1,0:T(8,128)S(1)}, u32[]{:S(2)}, u32[]{:S(2)}) collective-permute-start(f32[2,8,2048]{2,1,0:T(8,128)S(1)} %get-tuple-element.58), channel_id=1, source_target_pairs={{2,0},{4,2},{6,4},{8,6},{10,8},{12,10},{14,12},{16,14},{18,16},{20... | collective-permute-start | bytes 393224 | tf_op jit(solution)/shard_map/ppermute | solution.py:528
  92.1 37.8 %all-to-all-done.1.data = f32[16,2,128,128]{3,2,1,0:T(8,128)S(1)} async-done(((f32[16,2,128,128]{3,2,1,0:T(8,128)}), f32[16,2,128,128]{3,2,1,0:T(8,128)S(1)}, u32[]{:S(2)}, u32[]{:S(2)}) %all-to-all-start.1) | async-done | bytes 2097184 | tf_op jit(solution)/shard_map/all_to_all | solution.py:458
  129.9 1.3 copy-done.2
  131.2 6.0 %inverse_y.2 = (f32[128,2048]{1,0:T(8,128)}, f32[128,2048]{1,0:T(8,128)}) custom-call(f32[16,2,128,128]{3,2,1,0:T(8,128)} %copy-done.2, f32[16,2,256]{2,1,0:T(2,128)} %dynamic-slice_bitcast_fusion.turn, bf16[256,512]{1,0:T(8,128)(2,1)} %constant.38.clone.table_high, bf16[256,512]{1,0:T(8,128)(2,1)} %constant.39.clone.table_low), custom_call_target="tpu_custom_call" | custom-call | flops 1000000000 | bytes 4751360 | tf_op jit(solution)/shard_map/inverse_y/pallas_call | solution.py:414
  137.2 0.0 collective-permute-start.1
  137.2 1.0 fusion.5
  138.2 0.6 collective-permute-start.4
  138.8 0.0 copy-done.15
  138.8 0.0 copy-done.17
  138.8 0.8 select_reduce_fusion.4
  139.7 1.4 fusion.cells
  141.0 0.0 collective-permute-done.2.above
  141.0 0.0 collective-permute-done.3.below
  141.1 0.0 collective-permute-done.4.beside
  141.1 0.6 copy-done.10
  141.7 0.1 copy-done.11
  141.8 0.7 copy-done.8
  142.5 6.8 %stencil.2 = (f32[128,2048]{1,0:T(8,128)}, f32[128,2048]{1,0:T(8,128)}, f32[2,128,2048]{2,1,0:T(8,128)}, f32[128,2048]{1,0:T(8,128)}) custom-call(f32[2,128,2048]{2,1,0:T(8,128)} %previous.3, f32[2,128,2048]{2,1,0:T(8,128)} %previous.2, f32[128,2048]{1,0:T(8,128)} %slip.1, f32[4,8,2048]{2,1,0:T(8,128)} %fusion.cells, f32[2,8,2048]{2,1,0:T(8,128)} %copy-done.10, ...), custom_call_target="tpu_custom_call" | custom-call | flops 500000000 | bytes 11272192 | tf_op jit(solution)/shard_map/stencil/pallas_call | solution.py:414
  149.3 0.0 collective-permute-done.1.other
  149.3 1.0 copy-done.7
  150.2 4.6 %traction.2 = (f32[2,128,2048]{2,1,0:T(8,128)}, f32[128,2048]{1,0:T(8,128)}) custom-call(f32[128,2048]{1,0:T(8,128)} %get-tuple-element.30.own, f32[128,2048]{1,0:T(8,128)} %copy-done.7, f32[128,2048]{1,0:T(8,128)} %get-tuple-element.32.base, f32[128,2048]{1,0:T(8,128)} %get-tuple-element.33.strength, ...), custom_call_target="tpu_custom_call", output_to_operand_aliasing={{0}: (5, {})} | custom-call | tf_op jit(solution)/shard_map/traction/pallas_call | solution.py:541
  154.9 0.0 collective-permute-start.5
  154.9 2.8 collective-permute-done.5.other
  157.8 1.0 copy-done.6
  158.7 5.9 %forward_y.3 = f32[16,2,128,128]{3,2,1,0:T(8,128)} custom-call(f32[128,2048]{1,0:T(8,128)} %get-tuple-element.35.own, f32[128,2048]{1,0:T(8,128)} %copy-done.6, f32[16,2,256]{2,1,0:T(2,128)} %dynamic-slice_bitcast_fusion.turn, bf16[512,256]{1,0:T(8,128)(2,1)} %constant.36.clone.table_high, bf16[512,256]{1,0:T(8,128)(2,1)} %constant.37.clone.table_low), custom_call_target="tpu_custom_call" | custom-call | flops 1000000000 | bytes 4751360 | tf_op jit(solution)/shard_map/forward_y/pallas_call | solution.py:414
  164.6 58.8 %all_to_all.20.data = f32[16,2,128,128]{3,2,1,0:T(8,128)} all-to-all(f32[16,2,128,128]{3,2,1,0:T(8,128)} %forward_y.3), channel_id=1, replica_groups=mesh['groups'=1,'row'=16,'col'=2] {'row'}, dimensions={0} | all-to-all | bytes 4194304 | tf_op jit(solution)/shard_map/all_to_all | solution.py:458
  223.5 7.9 %middle.3 = f32[16,2,128,128]{3,2,1,0:T(8,128)} custom-call(f32[16,2,128,128]{3,2,1,0:T(8,128)} %all_to_all.20.data, f32[16,2,128]{2,1,0:T(2,128)} %constant.45.clone.turn, bf16[256,256]{1,0:T(8,128)(2,1)} %constant.40.clone.forward_high, bf16[256,256]{1,0:T(8,128)(2,1)} %constant.41.clone.forward_low, bf16[256,256]{1,0:T(8,128)(2,1)} %constant.42.clone.inverse_high, ...), custom_call_target="tpu_custom_call" | custom-call | flops 1000000000 | bytes 7880704 | tf_op jit(solution)/shard_map/middle/pallas_call | solution.py:414
  231.4 52.6 %all_to_all.21.data = f32[16,2,128,128]{3,2,1,0:T(8,128)} all-to-all(f32[16,2,128,128]{3,2,1,0:T(8,128)} %middle.3), channel_id=1, replica_groups=mesh['groups'=1,'row'=16,'col'=2] {'row'}, dimensions={0} | all-to-all | bytes 4194304 | tf_op jit(solution)/shard_map/all_to_all | solution.py:458
  284.0 6.0 %inverse_y.3 = (f32[128,2048]{1,0:T(8,128)}, f32[128,2048]{1,0:T(8,128)}) custom-call(f32[16,2,128,128]{3,2,1,0:T(8,128)} %all_to_all.21.data, f32[16,2,256]{2,1,0:T(2,128)} %dynamic-slice_bitcast_fusion.turn, bf16[256,512]{1,0:T(8,128)(2,1)} %constant.38.clone.table_high, bf16[256,512]{1,0:T(8,128)(2,1)} %constant.39.clone.table_low), custom_call_target="tpu_custom_call" | custom-call | flops 1000000000 | bytes 4751360 | tf_op jit(solution)/shard_map/inverse_y/pallas_call | solution.py:414
  290.0 0.0 collective-permute-start.6
  290.0 1.0 fusion.3
  291.0 0.6 collective-permute-start.9
  291.6 1.0 fusion.4
  292.5 0.6 collective-permute-start.7
  293.2 5.1 %collective-permute-start.8 = (f32[2,8,2048]{2,1,0:T(8,128)S(1)}, f32[2,8,2048]{2,1,0:T(8,128)S(1)}, u32[]{:S(2)}, u32[]{:S(2)}) collective-permute-start(f32[2,8,2048]{2,1,0:T(8,128)S(1)} %get-tuple-element.54), channel_id=1, source_target_pairs={{2,0},{4,2},{6,4},{8,6},{10,8},{12,10},{14,12},{16,14},{18,16},{20... | collective-permute-start | bytes 393224 | tf_op jit(solution)/shard_map/ppermute | solution.py:528
  298.2 3.5 %collective-permute-done.7.above = f32[2,8,2048]{2,1,0:T(8,128)S(1)} collective-permute-done((f32[2,8,2048]{2,1,0:T(8,128)S(1)}, f32[2,8,2048]{2,1,0:T(8,128)S(1)}, u32[]{:S(2)}, u32[]{:S(2)}) %collective-permute-start.7) | collective-permute-done | bytes 131104 | tf_op jit(solution)/shard_map/ppermute | solution.py:527
  301.7 0.0 collective-permute-done.8.below
  301.7 0.0 collective-permute-done.9.beside
  301.7 0.6 copy-done.12
  302.4 0.1 copy-done.13
  302.4 0.1 copy-done.9
  302.5 6.9 %stencil.3 = (f32[128,2048]{1,0:T(8,128)}, f32[128,2048]{1,0:T(8,128)}, f32[2,128,2048]{2,1,0:T(8,128)}, f32[128,2048]{1,0:T(8,128)}) custom-call(f32[2,128,2048]{2,1,0:T(8,128)} %get-tuple-element.39.current, f32[2,128,2048]{2,1,0:T(8,128)} %previous.3, f32[128,2048]{1,0:T(8,128)} %get-tuple-element.40.slip, f32[4,8,2048]{2,1,0:T(8,128)} %fusion.cells, ...), custom_call_target="tpu_custom_call" | custom-call | flops 500000000 | bytes 11272192 | tf_op jit(solution)/shard_map/stencil/pallas_call | solution.py:414
  309.4 0.0 collective-permute-done.6.other
  309.4 1.0 copy-done.4
  310.4 4.3 %traction.3 = (f32[2,128,2048]{2,1,0:T(8,128)}, f32[128,2048]{1,0:T(8,128)}) custom-call(f32[128,2048]{1,0:T(8,128)} %get-tuple-element.37.own, f32[128,2048]{1,0:T(8,128)} %copy-done.4, f32[128,2048]{1,0:T(8,128)} %get-tuple-element.41.base, f32[128,2048]{1,0:T(8,128)} %get-tuple-element.42.strength, ...), custom_call_target="tpu_custom_call", output_to_operand_aliasing={{0}: (4, {})} | custom-call | tf_op jit(solution)/shard_map/traction/pallas_call | solution.py:541
  (23 shorter events, 0.1 us)
Async XLA Ops:
  0.6 2.3 copy-start.14
  2.3 2.9 copy-start.1
  2.3 2.8 collective-permute-start
  5.2 1.0 copy-start.5
  12.1 51.5 %all-to-all-start = ((f32[16,2,128,128]{3,2,1,0:T(8,128)}), f32[16,2,128,128]{3,2,1,0:T(8,128)S(1)}, u32[]{:S(2)}, u32[]{:S(2)}) async-start(f32[16,2,128,128]{3,2,1,0:T(8,128)} %forward_y.2), calls=%async_computation | async-start | bytes 4194304 | tf_op jit(solution)/shard_map/all_to_all | solution.py:458
  63.6 1.3 copy-start
  74.4 55.5 %all-to-all-start.1 = ((f32[16,2,128,128]{3,2,1,0:T(8,128)}), f32[16,2,128,128]{3,2,1,0:T(8,128)S(1)}, u32[]{:S(2)}, u32[]{:S(2)}) async-start(f32[16,2,128,128]{3,2,1,0:T(8,128)} %get-tuple-element.29), calls=%async_computation.1 | async-start | bytes 4194304 | tf_op jit(solution)/shard_map/all_to_all | solution.py:458
  86.2 54.8 %collective-permute-start.2 = (f32[2,8,2048]{2,1,0:T(8,128)}, f32[2,8,2048]{2,1,0:T(8,128)S(1)}, u32[]{:S(2)}, u32[]{:S(2)}) collective-permute-start(f32[2,8,2048]{2,1,0:T(8,128)} %get-tuple-element.59), channel_id=1, source_target_pairs={{0,2},{2,4},{4,6},{6,8},{8,10},{10,12},{12,14},{14,16},{16,18},{18... | collective-permute-start | bytes 393224 | tf_op jit(solution)/shard_map/ppermute | solution.py:527
  88.2 50.7 %copy-start.15 = (s32[8,128]{1,0:T(8,128)S(1)}, s32[8,128]{1,0:T(8,128)}, u32[]{:S(2)}) copy-start(s32[8,128]{1,0:T(8,128)} %param.25) | copy-start | bytes 12292
  88.2 50.7 %copy-start.16 = (f32[8]{0:T(128)S(1)}, f32[8]{0:T(128)}, u32[]{:S(2)}) copy-start(f32[8]{0:T(128)} %param.31) | copy-start | bytes 100
  88.2 50.7 %copy-start.17 = (f32[8]{0:T(128)S(1)}, f32[8]{0:T(128)}, u32[]{:S(2)}) copy-start(f32[8]{0:T(128)} %param.32) | copy-start | bytes 100
  88.2 50.7 %copy-start.18 = (f32[8]{0:T(128)S(1)}, f32[8]{0:T(128)}, u32[]{:S(2)}) copy-start(f32[8]{0:T(128)} %param.30) | copy-start | bytes 100
  88.2 51.5 %copy-start.3 = (f32[128,2048,1]{1,0,2:T(8,128)S(1)}, f32[128,2048,1]{1,0,2:T(8,128)}, u32[]{:S(2)}) copy-start(f32[128,2048,1]{1,0,2:T(8,128)} %constant.48) | copy-start | bytes 3145732
  88.2 52.9 %collective-permute-start.3 = (f32[2,8,2048]{2,1,0:T(8,128)S(1)}, f32[2,8,2048]{2,1,0:T(8,128)S(1)}, u32[]{:S(2)}, u32[]{:S(2)}) collective-permute-start(f32[2,8,2048]{2,1,0:T(8,128)S(1)} %get-tuple-element.58), channel_id=1, source_target_pairs={{2,0},{4,2},{6,4},{8,6},{10,8},{12,10},{14,12},{16,14},{18,16},{20... | collective-permute-start | bytes 393224 | tf_op jit(solution)/shard_map/ppermute | solution.py:528
  129.9 1.3 copy-start.2
  137.2 12.1 %collective-permute-start.1 = (f32[128,2048]{1,0:T(8,128)}, f32[128,2048]{1,0:T(8,128)S(1)}, u32[]{:S(2)}, u32[]{:S(2)}) collective-permute-start(f32[128,2048]{1,0:T(8,128)} %get-tuple-element.31), channel_id=1, source_target_pairs={{0,1},{1,0},{2,3},{3,2},{4,5},{5,4},{6,7},{7,6},{8,9},{9,8},{10,11... | collective-permute-start | bytes 3145736 | tf_op jit(solution)/shard_map/ppermute | solution.py:455
  138.2 2.8 collective-permute-start.4
  141.0 0.7 copy-start.10
  141.1 0.7 copy-start.11
  141.8 0.7 copy-start.8
  149.3 1.0 copy-start.7
  154.9 2.9 collective-permute-start.5
  157.8 1.0 copy-start.6
  290.0 19.4 %collective-permute-start.6 = (f32[128,2048]{1,0:T(8,128)}, f32[128,2048]{1,0:T(8,128)S(1)}, u32[]{:S(2)}, u32[]{:S(2)}) collective-permute-start(f32[128,2048]{1,0:T(8,128)} %get-tuple-element.38), channel_id=1, source_target_pairs={{0,1},{1,0},{2,3},{3,2},{4,5},{5,4},{6,7},{7,6},{8,9},{9,8},{10,11... | collective-permute-start | bytes 3145736 | tf_op jit(solution)/shard_map/ppermute | solution.py:455
  291.0 10.7 %collective-permute-start.9 = (f32[2,128,256]{2,1,0:T(8,128)S(1)}, f32[2,128,256]{2,1,0:T(8,128)S(1)}, u32[]{:S(2)}, u32[]{:S(2)}) collective-permute-start(f32[2,128,256]{2,1,0:T(8,128)S(1)} %pad_maximum_fusion.1), channel_id=1, source_target_pairs={{0,1},{1,0},{2,3},{3,2},{4,5},{5,4},{6,7},{7,6},{8,9},{9,8},{10,11... | collective-permute-start | bytes 786440 | tf_op jit(solution)/shard_map/ppermute | solution.py:455
  292.5 9.2 %collective-permute-start.7 = (f32[2,8,2048]{2,1,0:T(8,128)S(1)}, f32[2,8,2048]{2,1,0:T(8,128)S(1)}, u32[]{:S(2)}, u32[]{:S(2)}) collective-permute-start(f32[2,8,2048]{2,1,0:T(8,128)S(1)} %get-tuple-element.55), channel_id=1, source_target_pairs={{0,2},{2,4},{4,6},{6,8},{8,10},{10,12},{12,14},{14,16},{16,18},{18... | collective-permute-start | bytes 393224 | tf_op jit(solution)/shard_map/ppermute | solution.py:527
  293.2 8.6 %collective-permute-start.8 = (f32[2,8,2048]{2,1,0:T(8,128)S(1)}, f32[2,8,2048]{2,1,0:T(8,128)S(1)}, u32[]{:S(2)}, u32[]{:S(2)}) collective-permute-start(f32[2,8,2048]{2,1,0:T(8,128)S(1)} %get-tuple-element.54), channel_id=1, source_target_pairs={{2,0},{4,2},{6,4},{8,6},{10,8},{12,10},{14,12},{16,14},{18,16},{20... | collective-permute-start | bytes 393224 | tf_op jit(solution)/shard_map/ppermute | solution.py:528
  301.7 0.6 copy-start.12
  301.7 0.7 copy-start.13
  301.7 0.8 copy-start.9
  309.4 1.0 copy-start.4

commit v2 on v1

--- a/solution.py
+++ b/solution.py
@@ -137,11 +137,9 @@
     q = (np.arange(row_count)[:, None] * (col_count * SUB) + np.arange(SUB)[None, :]).reshape(-1)
     angle = 2 * np.pi * np.outer(m, q) / m_count
     forward_y = halves(complex_block(np.cos(angle), -np.sin(angle)))
-    inverse_y = halves(complex_block(np.cos(angle.T), np.sin(angle.T)))
     i = np.arange(rows)
     angle = 2 * np.pi * np.outer(i, i) / rows
     forward_x = halves(complex_block(np.cos(angle), -np.sin(angle)))
-    inverse_x = halves(complex_block(np.cos(angle), np.sin(angle)))
     k = np.arange(n_count)
     col = np.arange(col_count)[:, None, None]
     angle = 2 * np.pi * (k[:, None] * m[None, :] / width + col * SUB * m[None, None, :] / m_count)
@@ -152,10 +150,8 @@
     angle = 2 * np.pi * np.outer(k, i) / length
     turn_x = np.stack([np.cos(angle), np.sin(angle)], 1) / math.sqrt(length)
     return dict(
-        forward_y=forward_y,
-        inverse_y=inverse_y,
-        forward_x=forward_x,
-        inverse_x=inverse_x,
+        table_y=forward_y,
+        table_x=forward_x,
         turn_y=jnp.asarray(turn_y, f32),
         turn_x=jnp.asarray(turn_x, f32),
     )
@@ -166,9 +162,12 @@
     return high, (z - high.astype(f32)).astype(bf16)
 
 
-def product(z, table_high, table_low):
+def product(z, table_high, table_low, inverse=False):
     high, low = split(z)
-    dot = functools.partial(jnp.dot, preferred_element_type=f32)
+
+    def dot(a, b):
+        return lax.dot_general(a, b, (((1,), (1 if inverse else 0,)), ((), ())), preferred_element_type=f32)
+
     return dot(high, table_high) + dot(low, table_high) + dot(high, table_low)
 
 
@@ -225,7 +224,7 @@
 
 
 def middle_kernel(
-    last, data, turn, forward_high, forward_low, inverse_high, inverse_low, first_kernel, load, *rest
+    last, data, turn, table_high, table_low, first_kernel, load, *rest
 ):
     if last:
         out, work = rest
@@ -246,7 +245,7 @@
     group = group_of(row_count, span)
     for g in range(0, row_count, group):
         z = work[g : g + group].reshape(group * span, 2 * rows)
-        spectrum = product(z, forward_high[...], forward_low[...]).reshape(group, span, 2 * rows)
+        spectrum = product(z, table_high[...], table_low[...]).reshape(group, span, 2 * rows)
         parts = (spectrum[:, :, :rows], spectrum[:, :, rows:])
         factor = first_kernel[g : g + group]
         loads = [load[c, g : g + group] + factor * parts[c] for c in range(2)]
@@ -255,7 +254,7 @@
             for c in range(2):
                 later_out[c, g : g + group] = later_load[c, g : g + group] + factor * parts[c]
         w = jnp.concatenate(loads, axis=2).reshape(group * span, 2 * rows)
-        w = product(w, inverse_high[...], inverse_low[...])
+        w = product(w, table_high[...], table_low[...], True)
         work[g : g + group] = w.reshape(group, span, 2 * rows)
 
     def scatter(t, carry):
@@ -287,7 +286,7 @@
             parts = [data[:, c, k * SUB : (k + 1) * SUB, :].reshape(q_count, rows).T for c in range(2)]
             blocks.append(jnp.concatenate(parts, axis=1))
         z = jnp.concatenate(blocks, axis=0)
-        o = product(z, table_high[...], table_low[...])
+        o = product(z, table_high[...], table_low[...], True)
         work[g : g + group] = o.reshape(group, rows, 2 * m_count)
 
     def tile(t, carry):
@@ -358,13 +357,16 @@
         reorder(5, second)
 
 
-def stencil_kernel(current, previous, slip, cells, above, below, beside, base, strength, following, grown):
+def stencil_kernel(
+    lower, upper, old_lower, old_upper, slip, cells, above, below, beside, base, strength, partial, following, grown
+):
     rows, cols = slip.shape
     lane = beside.shape[2] // 2
     row_index = lax.broadcasted_iota(jnp.int32, (rows, cols), 0)
     col_index = lax.broadcasted_iota(jnp.int32, (rows, cols), 1)
-    for layer in range(2):
-        here = current[layer]
+    layers = ((lower, old_lower, upper, partial), (upper, old_upper, lower, following))
+    for layer, (now, before, across, target) in enumerate(layers):
+        here = now[0]
         up = pltpu.roll(here, 1, 0)
         up = jnp.where(row_index == 0, above[layer, SUB - 1 : SUB, :], up)
         down = pltpu.roll(here, rows - 1, 0)
@@ -374,15 +376,11 @@
         right = pltpu.roll(here, cols - 1, 1)
         right = jnp.where(col_index == cols - 1, beside[layer, :, 0:1], right)
         flat = up + down + left + right - 4.0 * here
-        if layer == 0:
-            across = current[1] + here - 2.0 * here
-        else:
-            across = current[0] - 2.0 * here
-        following[layer] = 2.0 * here - previous[layer] + courant * (flat + across)
-    count = cells.shape[1]
-    for r in range(count):
+        normal = across[0] - 2.0 * here if layer else across[0] + here - 2.0 * here
+        target[0] = 2.0 * here - before[0] + courant * (flat + normal)
+    for r in range(cells.shape[1]):
         at = slice(r * BLOCK_CELLS, (r + 1) * BLOCK_CELLS)
-        rate = current[0, at, :] - previous[0, at, :]
+        rate = lower[0, at, :] - old_lower[0, at, :]
         old = slip[at, :]
         base[at, :] = cells[3, r : r + 1, :] - damping * rate
         weak = jnp.minimum(old * cells[2, r : r + 1, :], 1.0)
@@ -390,17 +388,19 @@
         grown[at, :] = old + jnp.abs(rate)
 
 
-def traction_kernel(own, other, base, strength, current, partial, following, result):
+def clipped(own, other, base, strength):
     limit = strength[...]
-    traction = jnp.clip(base[...] + (own[...] + other[...]), -limit, limit)
-    updated = partial[0] + courant * traction
+    return jnp.clip(base[...] + (own[...] + other[...]), -limit, limit)
+
+
+def traction_kernel(own, other, base, strength, partial, current, following, rate):
+    updated = partial[0] + courant * clipped(own, other, base, strength)
     following[0] = updated
-    result[...] = updated - current[0]
-
-
-def last_traction_kernel(own, other, base, strength, partial, following, result):
-    limit = strength[...]
-    traction = jnp.clip(base[...] + (own[...] + other[...]), -limit, limit)
+    rate[...] = updated - current[0]
+
+
+def last_traction_kernel(own, other, base, strength, partial, whole, following, result):
+    traction = clipped(own, other, base, strength)
     result[...] = traction
     following[0] = partial[0] + courant * traction
 
@@ -409,7 +409,7 @@
     return pl.BlockSpec(memory_space=pltpu.VMEM)
 
 
-def call(kernel, inputs, outputs, scratch=(), flops=0, name=None):
+def call(kernel, inputs, outputs, scratch=(), flops=0, name=None, limit=20 * 2**20):
     size = sum(int(np.prod(v.shape)) * v.dtype.itemsize for v in (*inputs, *outputs))
     return pl.pallas_call(
         kernel,
@@ -419,6 +419,7 @@
         scratch_shapes=list(scratch),
         cost_estimate=pl.CostEstimate(flops=flops, transcendentals=0, bytes_accessed=size),
         name=name,
+        compiler_params=pltpu.CompilerParams(vmem_limit_bytes=limit),
     )(*inputs)
 
 
@@ -472,7 +473,8 @@
             lookup(initial_stress),
         ]
     )
-    spread = np.repeat(np.eye(region_ids.shape[1], dtype=np.float32), BLOCK_CELLS, axis=1)
+    block_of = lax.broadcasted_iota(jnp.int32, (region_ids.shape[1], cols), 1) // BLOCK_CELLS
+    spread = (block_of == lax.broadcasted_iota(jnp.int32, block_of.shape, 0)).astype(f32)
     cells = jnp.einsum("abc,cd->abd", blocks, spread, precision=lax.Precision.HIGHEST)
 
     block = 16
@@ -494,11 +496,12 @@
             flops=20 * horizon * span * length, transcendentals=0, bytes_accessed=6 * horizon * span * length
         ),
         name="past_loads",
+        compiler_params=pltpu.CompilerParams(vmem_limit_bytes=32 * 2**20),
     )(wave_kernel, mode_history)
 
     def forward(rate):
         work = pltpu.VMEM((n_count, rows, 2 * m_count), f32)
-        inputs = (rate, swap(rate), turn_y, *tables["forward_y"])
+        inputs = (rate, swap(rate), turn_y, *tables["table_y"])
         (part,) = call(
             functools.partial(forward_y_kernel, n_count), inputs, [half_shape], [work], 10**9, "forward_y"
         )
@@ -507,14 +510,14 @@
     def middle(last, data, *more):
         work = pltpu.VMEM((row_count, span, 2 * rows), f32)
         outputs = [half_shape] if last else [half_shape, load_shape]
-        inputs = (data, tables["turn_x"], *tables["forward_x"], *tables["inverse_x"], *more)
+        inputs = (data, tables["turn_x"], *tables["table_x"], *more)
         return call(functools.partial(middle_kernel, last), inputs, outputs, [work], 10**9, "middle")
 
     def inverse(data):
         work = pltpu.VMEM((n_count, rows, 2 * m_count), f32)
         own, other = call(
             functools.partial(inverse_y_kernel, n_count),
-            (data, turn_y, *tables["inverse_y"]),
+            (data, turn_y, *tables["table_y"]),
             [tile_shape, tile_shape],
             [work],
             10**9,
@@ -522,43 +525,70 @@
         )
         return own, swap(other)
 
-    def stencil(current, previous, slip):
-        ring = [(i, (i + 1) % row_count) for i in range(row_count)]
-        above = lax.ppermute(current[:, rows - SUB :], "row", ring)
-        below = lax.ppermute(current[:, :SUB], "row", [(b, a) for a, b in ring])
-        edge = lane_width(cols)
-        beside = swap(jnp.concatenate([current[:, :, :edge], current[:, :, cols - edge :]], axis=2))
-        inputs = (current, previous, slip, cells, above, below, beside)
-        outputs = [tile_shape, tile_shape, jax.ShapeDtypeStruct(current.shape, f32), tile_shape]
-        return call(stencil_kernel, inputs, outputs, (), 5 * 10**8, "stencil")
-
-    def traction_step(kernel, *inputs):
+    ring = [(i, (i + 1) % row_count) for i in range(row_count)]
+    edge = lane_width(cols)
+    layer_shape = jax.ShapeDtypeStruct((1, rows, cols), f32)
+
+    def stencil(last, lower, upper, old_lower, old_upper, slip):
+        def edges(begin, size, axis):
+            pick = lambda v: lax.slice_in_dim(v[0][v[1] : v[1] + 1], begin, begin + size, axis=axis)
+            return jnp.concatenate([pick(lower), pick(upper)], axis=0)
+
+        above = lax.ppermute(edges(rows - SUB, SUB, 1), "row", ring)
+        below = lax.ppermute(edges(0, SUB, 1), "row", [(b, a) for a, b in ring])
+        beside = swap(jnp.concatenate([edges(0, edge, 2), edges(cols - edge, edge, 2)], axis=2))
+        layers = (lower, upper, old_lower, old_upper)
+        more = (slip, cells, above, below, beside)
+
+        def at_layer(index):
+            return pl.BlockSpec((1, rows, cols), lambda i: (index, 0, 0))
+
+        following = jax.ShapeDtypeStruct((2, rows, cols), f32) if last else layer_shape
+        specs = [tile_shape, tile_shape, layer_shape, following, tile_shape]
+        whole = pl.BlockSpec((rows, cols), lambda i: (0, 0))
+        return pl.pallas_call(
+            stencil_kernel,
+            grid=(1,),
+            in_specs=[at_layer(index) for _, index in layers] + [vmem()] * len(more),
+            out_specs=[whole, whole, at_layer(0), at_layer(1 if last else 0), whole],
+            out_shape=specs,
+            cost_estimate=pl.CostEstimate(flops=5 * 10**9, transcendentals=0, bytes_accessed=40 * rows * cols),
+            compiler_params=pltpu.CompilerParams(vmem_limit_bytes=40 * 2**20),
+            name="stencil",
+        )(*[v for v, _ in layers], *more)
+
+    def traction_step(last, own, other, base, strength, partial, extra):
         step = 32 if rows % 32 == 0 else rows
         layer = pl.BlockSpec((1, step, cols), lambda i: (0, i, 0))
         tile = pl.BlockSpec((step, cols), lambda i: (i, 0))
-        partial = inputs[-1]
-        specs = [layer if v.ndim == 3 else tile for v in inputs]
         return pl.pallas_call(
-            kernel,
+            last_traction_kernel if last else traction_kernel,
             grid=(rows // step,),
-            in_specs=specs,
+            in_specs=[tile] * 4 + [layer, pl.BlockSpec(memory_space=pl.ANY) if last else layer],
             out_specs=[layer, tile],
-            out_shape=[jax.ShapeDtypeStruct(partial.shape, f32), tile_shape],
-            input_output_aliases={len(inputs) - 1: 0},
+            out_shape=[jax.ShapeDtypeStruct(extra.shape if last else (1, rows, cols), f32), tile_shape],
+            input_output_aliases={5: 0} if last else {},
+            compiler_params=pltpu.CompilerParams(vmem_limit_bytes=12 * 2**20),
             name="traction",
-        )(*inputs)
+        )(own, other, base, strength, partial, extra)
 
     data = forward(wave_now[0] - wave_before[0])
-    base, strength, partial, slip = stencil(wave_now, wave_before, fault_slip)
+    found = stencil(False, (wave_now, 0), (wave_now, 1), (wave_before, 0), (wave_before, 1), fault_slip)
+    data, (loads, later_loads, first, second), found = lax.optimization_barrier(
+        (data, (loads, later_loads, first, second), found)
+    )
+    base, strength, partial, upper, slip = found
     back, later_loads = middle(False, data, first, loads, second, later_loads)
     own, other = inverse(regroup(back))
-    current, rate = traction_step(traction_kernel, own, other, base, strength, wave_now, partial)
+    lower, rate = traction_step(False, own, other, base, strength, partial, wave_now)
 
     data = forward(rate)
-    base, strength, partial, slip = stencil(current, wave_now, slip)
+    found = stencil(True, (lower, 0), (upper, 0), (wave_now, 0), (wave_now, 1), slip)
+    data, found = lax.optimization_barrier((data, found))
+    base, strength, partial, following, slip = found
     (back,) = middle(True, data, first, later_loads)
     own, other = inverse(regroup(back))
-    current, traction = traction_step(last_traction_kernel, own, other, base, strength, partial)
+    current, traction = traction_step(True, own, other, base, strength, partial, following)
     return (current, slip, traction)
 
 

time: 316 us -> 288 us (0.911)
  Pallas kernels: 84.7 us -> 46.8 us
  local copies, waits for them, and re-layouts: 14 us -> 36.2 us
  waiting for transfers between devices: 68.3 us -> 55.5 us
  blocking collectives: 111 us -> 121 us
  starting transfers between devices: 31.7 us -> 24.6 us
    all_to_all x2, waiting for transfers between devices: 60.3 us -> 0.01 us  [regroup(): return lax.all_to_all(value, 'row', split_axis=0, concat_axis=0, tiled=True)]
    ppermute x4, waiting for transfers between devices: 3.5 us -> 45.4 us  [the longest x2 40.2 us: stencil(): above = lax.ppermute(edges(rows - SUB, SUB, 1), 'row', ring)]
    pallas_call x8 -> x6, Pallas kernels: 55 us -> 22.2 us  [call(): pl.pallas_call(kernel, in_specs=[vmem()] * len(inputs), out_specs=[vmem()...]
    unnamed x38 -> x104, local copies, waits for them, and re-layouts: 8.75 us -> 30.5 us
    all_to_all x2, blocking collectives: 111 us -> 121 us  [regroup(): return lax.all_to_all(value, 'row', split_axis=0, concat_axis=0, tiled=True)]
    all_to_all x2, starting transfers between devices: 18.4 us -> 12.3 us  [regroup(): return lax.all_to_all(value, 'row', split_axis=0, concat_axis=0, tiled=True)]
    ppermute x6, waiting for transfers between devices: 4.51 us -> 10.1 us  [swap(): return lax.ppermute(value, 'col', [(0, 1), (1, 0)])]
    pallas_call x1, Pallas kernels: 20.7 us -> 17 us  [shards(): pl.pallas_call(load_kernel, grid=(span // block,), in_specs=[pl.BlockSpec...]
  transfers between devices with their start and end apart: 12 -> 12, of which waited for: 5 -> 7; matrix products, arithmetic and copies ran while one was open for 2% -> 2% of each run, Pallas kernels for 13% -> 8%
where the time goes in v2:
time: 288 us; the launch traced here: 287 us
  blocking collectives  121 us (42%)
  waiting for transfers between devices  55.5 us (19%)
  Pallas kernels  46.8 us (16%)
  local copies, waits for them, and re-layouts  36.2 us (13%)
  starting transfers between devices  24.6 us (9%)
    all_to_all x2, blocking collectives, regroup(): return lax.all_to_all(value, 'row', split_axis=0, concat_axis=0, tiled=True)  121 us
    ppermute x2, waiting for transfers between devices, stencil(): above = lax.ppermute(edges(rows - SUB, SUB, 1), 'row', ring)  40.2 us
    unnamed x104, local copies, waits for them, and re-layouts  30.5 us
    pallas_call x6, Pallas kernels, call(): pl.pallas_call(kernel, in_specs=[vmem()] * len(inputs), out_specs=[vmem()...  22.2 us
    pallas_call x1, Pallas kernels, shards(): pl.pallas_call(load_kernel, grid=(span // block,), in_specs=[pl.BlockSpec...  17 us
    all_to_all x2, starting transfers between devices, regroup(): return lax.all_to_all(value, 'row', split_axis=0, concat_axis=0, tiled=True)  12.3 us
    ppermute x6, waiting for transfers between devices, swap(): return lax.ppermute(value, 'col', [(0, 1), (1, 0)])  10.1 us
    ppermute x2, starting transfers between devices, stencil(): below = lax.ppermute(edges(0, SUB, 1), 'row', [(b, a) for a, b in ring])  9.33 us
  transfers between devices with their start and end apart: 12, of which 7 were waited for; matrix products, arithmetic and copies ran while one was open for 2% of the time, Pallas kernels for 8%

profile of v2, /device:TPU:0, one launch (start us, length us, event | category | flops | bytes accessed | tf_op | source)
XLA Modules:
  0.0 287.3 jit_solution(9445665280519065995)
XLA Ops:
  0.7 1.7 subtract_bitcast_fusion.own
  2.4 0.6 collective-permute-start
  3.0 2.3 collective-permute-done.other
  5.2 4.3 %forward_y.2 = f32[16,2,128,128]{3,2,1,0:T(8,128)} custom-call(f32[128,2048]{1,0:T(8,128)S(1)} %subtract_bitcast_fusion.own, f32[128,2048]{1,0:T(8,128)S(1)} %collective-permute-done.other, f32[16,2,256]{2,1,0:T(2,128)S(1)} %dynamic-slice_bitcast_fusion.turn, bf16[512,256]{1,0:T(8,128)(2,1)S(1)} %copy-done.25, bf16[512,256]{1,0:T(8,128)(2,1)S(1)} %copy-done.24), custom_call_target="tpu_custom_call" | custom-call | flops 1000000000 | bytes 4751360 | tf_op jit(solution)/shard_map/forward_y/pallas_call | solution.py:414
  9.5 8.4 %all-to-all-start = ((f32[16,2,128,128]{3,2,1,0:T(8,128)}), f32[16,2,128,128]{3,2,1,0:T(8,128)S(1)}, u32[]{:S(2)}, u32[]{:S(2)}) async-start(f32[16,2,128,128]{3,2,1,0:T(8,128)} %forward_y.2), calls=%async_computation | async-start | bytes 4194304 | tf_op jit(solution)/shard_map/all_to_all | solution.py:459
  17.9 1.0 fusion.19
  18.9 5.6 %collective-permute-start.2 = (f32[2,8,2048]{2,1,0:T(8,128)S(1)}, f32[2,8,2048]{2,1,0:T(8,128)S(1)}, u32[]{:S(2)}, u32[]{:S(2)}) collective-permute-start(f32[2,8,2048]{2,1,0:T(8,128)S(1)} %get-tuple-element.90), channel_id=1, source_target_pairs={{2,0},{4,2},{6,4},{8,6},{10,8},{12,10},{14,12},{16,14},{18,16},{20... | collective-permute-start | bytes 393224 | tf_op jit(solution)/shard_map/ppermute | solution.py:538
  24.5 1.0 fusion.18
  25.5 0.1 collective-permute-start.3
  25.7 0.1 select_reduce_fusion.4
  25.8 3.4 %copy-done = bf16[16,128,2048]{2,1,0:T(8,128)(2,1)S(1)} copy-done((bf16[16,128,2048]{2,1,0:T(8,128)(2,1)S(1)}, bf16[16,128,2048]{2,1,0:T(8,128)(2,1)}, u32[]{:S(2)}) %copy-start) | copy-done | bytes 8388632
  29.2 17.0 %past_loads.1 = (f32[2,16,128,128]{3,2,1,0:T(8,128)S(1)}, f32[2,16,128,128]{3,2,1,0:T(8,128)S(1)}, f32[16,128,128]{2,1,0:T(8,128)S(1)}, f32[16,128,128]{2,1,0:T(8,128)S(1)}) custom-call(bf16[16,128,2048]{2,1,0:T(8,128)(2,1)S(1)} %copy-done, bf16[16,2,128,2048]{3,2,1,0:T(8,128)(2,1)} %history.1), custom_call_target="tpu_custom_call" | custom-call | flops 83886080 | bytes 25165824 | tf_op jit(solution)/shard_map/past_loads/pallas_call | solution.py:482
  46.2 1.3 copy-done.6
  47.5 1.3 copy-done.8
  48.9 1.0 copy-done.10
  49.8 0.5 fusion.1.cells
  50.3 5.2 %collective-permute-done.2.below = f32[2,8,2048]{2,1,0:T(8,128)S(1)} collective-permute-done((f32[2,8,2048]{2,1,0:T(8,128)S(1)}, f32[2,8,2048]{2,1,0:T(8,128)S(1)}, u32[]{:S(2)}, u32[]{:S(2)}) %collective-permute-start.2) | collective-permute-done | bytes 131104 | tf_op jit(solution)/shard_map/ppermute | solution.py:538
  55.5 6.0 %collective-permute-done.1.above = f32[2,8,2048]{2,1,0:T(8,128)S(1)} collective-permute-done((f32[2,8,2048]{2,1,0:T(8,128)S(1)}, f32[2,8,2048]{2,1,0:T(8,128)S(1)}, u32[]{:S(2)}, u32[]{:S(2)}) %collective-permute-start.1) | collective-permute-done | bytes 131104 | tf_op jit(solution)/shard_map/ppermute | solution.py:537
  61.6 2.1 stencil.2
  63.8 1.0 copy-done.18
  64.7 1.0 copy-done.20
  65.7 1.0 copy-done.22
  66.8 1.0 copy-done.36
  67.8 0.7 copy-done.41
  68.5 1.0 copy-done.43
  69.5 1.6 copy-done.7
  71.1 1.6 copy-done.9
  72.6 1.2 copy-done.11
  73.9 0.9 copy-done.30
  74.8 3.9 %middle.2 = (f32[16,2,128,128]{3,2,1,0:T(8,128)S(1)}, f32[2,16,128,128]{3,2,1,0:T(8,128)S(1)}) custom-call(f32[16,2,128,128]{3,2,1,0:T(8,128)S(1)} %all-to-all-done.data, f32[16,2,128]{2,1,0:T(2,128)S(1)} %copy-done.35, bf16[256,256]{1,0:T(8,128)(2,1)S(1)} %copy-done.30, bf16[256,256]{1,0:T(8,128)(2,1)S(1)} %copy-done.29, ...), custom_call_target="tpu_custom_call" | custom-call | flops 1000000000 | bytes 12861440 | tf_op jit(solution)/shard_map/middle/pallas_call | solution.py:414
  78.7 1.3 copy-done.4
  80.0 60.4 %all_to_all.20.data = f32[16,2,128,128]{3,2,1,0:T(8,128)S(1)} all-to-all(f32[16,2,128,128]{3,2,1,0:T(8,128)S(1)} %get-tuple-element.57), channel_id=1, replica_groups=mesh['groups'=1,'row'=16,'col'=2] {'row'}, dimensions={0} | all-to-all | bytes 4194304 | tf_op jit(solution)/shard_map/all_to_all | solution.py:459
  140.4 3.0 %inverse_y.2 = (f32[128,2048]{1,0:T(8,128)S(1)}, f32[128,2048]{1,0:T(8,128)S(1)}) custom-call(f32[16,2,128,128]{3,2,1,0:T(8,128)S(1)} %all_to_all.20.data, f32[16,2,256]{2,1,0:T(2,128)S(1)} %copy-done.33, bf16[512,256]{1,0:T(8,128)(2,1)S(1)} %copy-done.26, bf16[512,256]{1,0:T(8,128)(2,1)S(1)} %copy-done.24), custom_call_target="tpu_custom_call" | custom-call | flops 1000000000 | bytes 4751360 | tf_op jit(solution)/shard_map/inverse_y/pallas_call | solution.py:414
  143.4 0.1 collective-permute-start.4
  143.5 2.6 collective-permute-done.4.other
  146.2 0.4 traction.2
  146.6 1.0 copy-done.38
  147.6 0.1 collective-permute-start.5
  147.7 2.5 collective-permute-done.5.other
  150.2 4.3 %forward_y.3 = f32[16,2,128,128]{3,2,1,0:T(8,128)} custom-call(f32[128,2048]{1,0:T(8,128)S(1)} %get-tuple-element.63.own, f32[128,2048]{1,0:T(8,128)S(1)} %collective-permute-done.5.other, f32[16,2,256]{2,1,0:T(2,128)S(1)} %copy-done.33, bf16[512,256]{1,0:T(8,128)(2,1)S(1)} %copy-done.26, bf16[512,256]{1,0:T(8,128)(2,1)S(1)} %copy-done.24), custom_call_target="tpu_custom_call" | custom-call | flops 1000000000 | bytes 4751360 | tf_op jit(solution)/shard_map/forward_y/pallas_call | solution.py:414
  154.5 3.9 %all-to-all-start.2 = ((f32[16,2,128,128]{3,2,1,0:T(8,128)}), f32[16,2,128,128]{3,2,1,0:T(8,128)S(1)}, u32[]{:S(2)}, u32[]{:S(2)}) async-start(f32[16,2,128,128]{3,2,1,0:T(8,128)} %forward_y.3), calls=%async_computation.2 | async-start | bytes 4194304 | tf_op jit(solution)/shard_map/all_to_all | solution.py:459
  158.4 1.0 fusion.21
  159.5 0.9 fusion.23
  160.4 0.9 fusion.22
  161.3 2.0 collective-permute-start.6
  163.3 0.9 fusion.20
  164.3 3.8 %collective-permute-start.7 = (f32[2,8,2048]{2,1,0:T(8,128)S(1)}, f32[2,8,2048]{2,1,0:T(8,128)S(1)}, u32[]{:S(2)}, u32[]{:S(2)}) collective-permute-start(f32[2,8,2048]{2,1,0:T(8,128)S(1)} %pad_maximum_fusion.2), channel_id=1, source_target_pairs={{2,0},{4,2},{6,4},{8,6},{10,8},{12,10},{14,12},{16,14},{18,16},{20... | collective-permute-start | bytes 393224 | tf_op jit(solution)/shard_map/ppermute | solution.py:538
  168.0 34.2 %collective-permute-done.6.above = f32[2,8,2048]{2,1,0:T(8,128)S(1)} collective-permute-done((f32[2,8,2048]{2,1,0:T(8,128)S(1)}, f32[2,8,2048]{2,1,0:T(8,128)S(1)}, u32[]{:S(2)}, u32[]{:S(2)}) %collective-permute-start.6) | collective-permute-done | bytes 131104 | tf_op jit(solution)/shard_map/ppermute | solution.py:537
  202.2 1.2 copy-done.37
  203.4 1.2 copy-done.39
  204.7 0.9 copy-done.42
  205.6 1.2 copy-done.44
  206.8 3.1 %stencil.3 = (f32[128,2048]{1,0:T(8,128)S(1)}, f32[128,2048]{1,0:T(8,128)S(1)}, f32[1,128,2048]{2,1,0:T(8,128)S(1)}, f32[2,128,2048]{2,1,0:T(8,128)}, f32[128,2048]{1,0:T(8,128)}) custom-call(f32[1,128,2048]{2,1,0:T(8,128)S(1)} %copy-done.39, f32[1,128,2048]{2,1,0:T(8,128)S(1)} %copy-done.37, f32[2,128,2048]{2,1,0:T(8,128)S(1)} %copy-done.3, ...), custom_call_target="tpu_custom_call" | custom-call | flops 5000000000 | bytes 10485760 | tf_op jit(solution)/shard_map/stencil/pallas_call | solution.py:549
  209.9 1.0 copy-done.12
  210.9 1.0 copy-done.14
  211.9 1.0 copy-done.16
  212.9 1.6 copy-done.5
  214.5 0.9 copy-done.31
  215.4 3.8 %middle.3 = f32[16,2,128,128]{3,2,1,0:T(8,128)S(1)} custom-call(f32[16,2,128,128]{3,2,1,0:T(8,128)S(1)} %all-to-all-done.2.data, f32[16,2,128]{2,1,0:T(2,128)S(1)} %copy-done.35, bf16[256,256]{1,0:T(8,128)(2,1)S(1)} %copy-done.31, bf16[256,256]{1,0:T(8,128)(2,1)S(1)} %copy-done.29, f32[16,128,128]{2,1,0:T(8,128)S(1)} %get-tuple-element.53.first_kernel, ...), custom_call_target="tpu_custom_call" | custom-call | flops 1000000000 | bytes 7618560 | tf_op jit(solution)/shard_map/middle/pallas_call | solution.py:414
  219.3 60.4 %all_to_all.21.data = f32[16,2,128,128]{3,2,1,0:T(8,128)S(1)} all-to-all(f32[16,2,128,128]{3,2,1,0:T(8,128)S(1)} %middle.3), channel_id=1, replica_groups=mesh['groups'=1,'row'=16,'col'=2] {'row'}, dimensions={0} | all-to-all | bytes 4194304 | tf_op jit(solution)/shard_map/all_to_all | solution.py:459
  279.7 3.0 %inverse_y.3 = (f32[128,2048]{1,0:T(8,128)S(1)}, f32[128,2048]{1,0:T(8,128)S(1)}) custom-call(f32[16,2,128,128]{3,2,1,0:T(8,128)S(1)} %all_to_all.21.data, f32[16,2,256]{2,1,0:T(2,128)S(1)} %copy-done.34, bf16[512,256]{1,0:T(8,128)(2,1)S(1)} %copy-done.27, bf16[512,256]{1,0:T(8,128)(2,1)S(1)} %copy-done.24), custom_call_target="tpu_custom_call" | custom-call | flops 1000000000 | bytes 4751360 | tf_op jit(solution)/shard_map/inverse_y/pallas_call | solution.py:414
  282.7 0.1 collective-permute-start.9
  282.7 2.6 collective-permute-done.9.other
  285.4 1.9 traction.3
  (95 shorter events, 0.4 us)
Async XLA Ops:
  0.6 2.3 copy-start.45
  0.6 4.6 %copy-start.24 = (bf16[512,256]{1,0:T(8,128)(2,1)S(1)}, bf16[512,256]{1,0:T(8,128)(2,1)}, u32[]{:S(2)}) copy-start(bf16[512,256]{1,0:T(8,128)(2,1)} %constant.46.clone.table_low) | copy-start | bytes 786436
  0.7 4.6 %copy-start.25 = (bf16[512,256]{1,0:T(8,128)(2,1)S(1)}, bf16[512,256]{1,0:T(8,128)(2,1)}, u32[]{:S(2)}) copy-start(bf16[512,256]{1,0:T(8,128)(2,1)} %constant.45.clone.table_high) | copy-start | bytes 786436
  2.4 2.8 collective-permute-start
  3.0 6.5 %copy-start.32 = (f32[16,2,256]{2,1,0:T(2,128)}, f32[16,2,256]{2,1,0:T(2,128)S(1)}, u32[]{:S(2)}) copy-start(f32[16,2,256]{2,1,0:T(2,128)S(1)} %dynamic-slice_bitcast_fusion.turn) | copy-start | bytes 98308
  9.5 16.1 %copy-start.46 = (s32[8,128]{1,0:T(8,128)S(1)}, s32[8,128]{1,0:T(8,128)}, u32[]{:S(2)}) copy-start(s32[8,128]{1,0:T(8,128)} %param.20) | copy-start | bytes 12292
  9.5 16.1 %copy-start.47 = (f32[8]{0:T(128)S(1)}, f32[8]{0:T(128)}, u32[]{:S(2)}) copy-start(f32[8]{0:T(128)} %param.26) | copy-start | bytes 100
  9.5 16.1 %copy-start.48 = (f32[8]{0:T(128)S(1)}, f32[8]{0:T(128)}, u32[]{:S(2)}) copy-start(f32[8]{0:T(128)} %param.27) | copy-start | bytes 100
  9.5 16.1 %copy-start.49 = (f32[8]{0:T(128)S(1)}, f32[8]{0:T(128)}, u32[]{:S(2)}) copy-start(f32[8]{0:T(128)} %param.25) | copy-start | bytes 100
  9.5 16.1 %copy-start.50 = (f32[8]{0:T(128)S(1)}, f32[8]{0:T(128)}, u32[]{:S(2)}) copy-start(f32[8]{0:T(128)} %param.24) | copy-start | bytes 100
  9.5 16.1 %copy-start.51 = (f32[8]{0:T(128)S(1)}, f32[8]{0:T(128)}, u32[]{:S(2)}) copy-start(f32[8]{0:T(128)} %param.23) | copy-start | bytes 100
  9.5 59.9 %all-to-all-start = ((f32[16,2,128,128]{3,2,1,0:T(8,128)}), f32[16,2,128,128]{3,2,1,0:T(8,128)S(1)}, u32[]{:S(2)}, u32[]{:S(2)}) async-start(f32[16,2,128,128]{3,2,1,0:T(8,128)} %forward_y.2), calls=%async_computation | async-start | bytes 4194304 | tf_op jit(solution)/shard_map/all_to_all | solution.py:459
  18.9 36.6 %collective-permute-start.2 = (f32[2,8,2048]{2,1,0:T(8,128)S(1)}, f32[2,8,2048]{2,1,0:T(8,128)S(1)}, u32[]{:S(2)}, u32[]{:S(2)}) collective-permute-start(f32[2,8,2048]{2,1,0:T(8,128)S(1)} %get-tuple-element.90), channel_id=1, source_target_pairs={{2,0},{4,2},{6,4},{8,6},{10,8},{12,10},{14,12},{16,14},{18,16},{20... | collective-permute-start | bytes 393224 | tf_op jit(solution)/shard_map/ppermute | solution.py:538
  24.5 37.1 %collective-permute-start.1 = (f32[2,8,2048]{2,1,0:T(8,128)S(1)}, f32[2,8,2048]{2,1,0:T(8,128)S(1)}, u32[]{:S(2)}, u32[]{:S(2)}) collective-permute-start(f32[2,8,2048]{2,1,0:T(8,128)S(1)} %get-tuple-element.91), channel_id=1, source_target_pairs={{0,2},{2,4},{4,6},{6,8},{8,10},{10,12},{12,14},{14,16},{16,18},{18... | collective-permute-start | bytes 393224 | tf_op jit(solution)/shard_map/ppermute | solution.py:537
  25.5 36.1 %collective-permute-start.3 = (f32[2,128,256]{2,1,0:T(8,128)S(1)}, f32[2,128,256]{2,1,0:T(8,128)S(1)}, u32[]{:S(2)}, u32[]{:S(2)}) collective-permute-start(f32[2,128,256]{2,1,0:T(8,128)S(1)} %pad_maximum_fusion), channel_id=1, source_target_pairs={{0,1},{1,0},{2,3},{3,2},{4,5},{5,4},{6,7},{7,6},{8,9},{9,8},{10,11... | collective-permute-start | bytes 786440 | tf_op jit(solution)/shard_map/ppermute | solution.py:456
  25.8 3.4 %copy-start = (bf16[16,128,2048]{2,1,0:T(8,128)(2,1)S(1)}, bf16[16,128,2048]{2,1,0:T(8,128)(2,1)}, u32[]{:S(2)}) copy-start(bf16[16,128,2048]{2,1,0:T(8,128)(2,1)} %kernel.1) | copy-start | bytes 25165828
  29.2 32.4 %copy-start.1 = (f32[2,128,2048]{2,1,0:T(8,128)S(1)}, f32[2,128,2048]{2,1,0:T(8,128)}, u32[]{:S(2)}) copy-start(f32[2,128,2048]{2,1,0:T(8,128)} %old_upper.3) | copy-start | bytes 6291460
  29.2 32.4 %copy-start.28 = (f32[2,128,2048]{2,1,0:T(8,128)S(1)}, f32[2,128,2048]{2,1,0:T(8,128)}, u32[]{:S(2)}) copy-start(f32[2,128,2048]{2,1,0:T(8,128)} %old_upper.2) | copy-start | bytes 6291460
  29.2 32.4 %copy-start.40 = (f32[128,2048]{1,0:T(8,128)S(1)}, f32[128,2048]{1,0:T(8,128)}, u32[]{:S(2)}) copy-start(f32[128,2048]{1,0:T(8,128)} %slip.1) | copy-start | bytes 3145732
  46.2 1.3 copy-start.6
  47.5 1.3 copy-start.8
  48.9 1.0 copy-start.10
  50.3 19.1 %copy-start.29 = (bf16[256,256]{1,0:T(8,128)(2,1)S(1)}, bf16[256,256]{1,0:T(8,128)(2,1)}, u32[]{:S(2)}) copy-start(bf16[256,256]{1,0:T(8,128)(2,1)} %constant.48.clone.table_low) | copy-start | bytes 393220
  50.3 19.1 %copy-start.35 = (f32[16,2,128]{2,1,0:T(2,128)S(1)}, f32[16,2,128]{2,1,0:T(2,128)}, u32[]{:S(2)}) copy-start(f32[16,2,128]{2,1,0:T(2,128)} %constant.50.clone.turn) | copy-start | bytes 49156
  63.7 1.0 copy-start.18
  64.7 1.0 copy-start.20
  65.7 1.0 copy-start.22
  66.7 1.0 copy-start.36
  67.8 0.7 copy-start.41
  68.5 1.0 copy-start.43
  69.5 1.6 copy-start.7
  71.1 1.6 copy-start.9
  72.6 1.2 copy-start.11
  73.9 0.9 copy-start.30
  78.7 1.3 copy-start.4
  80.0 60.4 %copy-start.26 = (bf16[512,256]{1,0:T(8,128)(2,1)S(1)}, bf16[512,256]{1,0:T(8,128)(2,1)}, u32[]{:S(2)}) copy-start(bf16[512,256]{1,0:T(8,128)(2,1)} %constant.45.clone.table_high) | copy-start | bytes 786436
  80.0 60.4 %copy-start.33 = (f32[16,2,256]{2,1,0:T(2,128)S(1)}, f32[16,2,256]{2,1,0:T(2,128)}, u32[]{:S(2)}) copy-start(f32[16,2,256]{2,1,0:T(2,128)} %copy-done.32) | copy-start | bytes 98308
  80.0 66.2 %copy-start.21 = (f32[128,2048]{1,0:T(8,128)S(1)}, f32[128,2048]{1,0:T(8,128)}, u32[]{:S(2)}) copy-start(f32[128,2048]{1,0:T(8,128)} %copy-done.20) | copy-start | bytes 3145732
  80.0 66.2 %copy-start.23 = (f32[1,128,2048]{2,1,0:T(8,128)S(1)}, f32[1,128,2048]{2,1,0:T(8,128)}, u32[]{:S(2)}) copy-start(f32[1,128,2048]{2,1,0:T(8,128)} %copy-done.22) | copy-start | bytes 3145732
  140.4 5.7 %copy-start.2 = (f32[2,128,2048]{2,1,0:T(8,128)S(1)}, f32[2,128,2048]{2,1,0:T(8,128)}, u32[]{:S(2)}) copy-start(f32[2,128,2048]{2,1,0:T(8,128)} %old_upper.3) | copy-start | bytes 6291460
  140.4 5.7 %copy-start.19 = (f32[128,2048]{1,0:T(8,128)S(1)}, f32[128,2048]{1,0:T(8,128)}, u32[]{:S(2)}) copy-start(f32[128,2048]{1,0:T(8,128)} %copy-done.18) | copy-start | bytes 3145732
  143.4 2.7 collective-permute-start.4
  146.6 1.0 copy-start.38
  147.6 2.7 collective-permute-start.5
  154.5 58.4 %all-to-all-start.2 = ((f32[16,2,128,128]{3,2,1,0:T(8,128)}), f32[16,2,128,128]{3,2,1,0:T(8,128)S(1)}, u32[]{:S(2)}, u32[]{:S(2)}) async-start(f32[16,2,128,128]{3,2,1,0:T(8,128)} %forward_y.3), calls=%async_computation.2 | async-start | bytes 4194304 | tf_op jit(solution)/shard_map/all_to_all | solution.py:459
  158.4 43.8 %copy-start.3 = (f32[2,128,2048]{2,1,0:T(8,128)S(1)}, f32[2,128,2048]{2,1,0:T(8,128)}, u32[]{:S(2)}) copy-start(f32[2,128,2048]{2,1,0:T(8,128)} %old_upper.3) | copy-start | bytes 6291460
  161.3 40.9 %collective-permute-start.6 = (f32[2,8,2048]{2,1,0:T(8,128)S(1)}, f32[2,8,2048]{2,1,0:T(8,128)S(1)}, u32[]{:S(2)}, u32[]{:S(2)}) collective-permute-start(f32[2,8,2048]{2,1,0:T(8,128)S(1)} %pad_maximum_fusion.1), channel_id=1, source_target_pairs={{0,2},{2,4},{4,6},{6,8},{8,10},{10,12},{12,14},{14,16},{16,18},{18... | collective-permute-start | bytes 393224 | tf_op jit(solution)/shard_map/ppermute | solution.py:537
  164.2 38.0 %collective-permute-start.8 = (f32[2,128,256]{2,1,0:T(8,128)S(1)}, f32[2,128,256]{2,1,0:T(8,128)S(1)}, u32[]{:S(2)}, u32[]{:S(2)}) collective-permute-start(f32[2,128,256]{2,1,0:T(8,128)S(1)} %maximum_maximum_fusion), channel_id=1, source_target_pairs={{0,1},{1,0},{2,3},{3,2},{4,5},{5,4},{6,7},{7,6},{8,9},{9,8},{10,11... | collective-permute-start | bytes 786440 | tf_op jit(solution)/shard_map/ppermute | solution.py:456
  164.3 37.9 %collective-permute-start.7 = (f32[2,8,2048]{2,1,0:T(8,128)S(1)}, f32[2,8,2048]{2,1,0:T(8,128)S(1)}, u32[]{:S(2)}, u32[]{:S(2)}) collective-permute-start(f32[2,8,2048]{2,1,0:T(8,128)S(1)} %pad_maximum_fusion.2), channel_id=1, source_target_pairs={{2,0},{4,2},{6,4},{8,6},{10,8},{12,10},{14,12},{16,14},{18,16},{20... | collective-permute-start | bytes 393224 | tf_op jit(solution)/shard_map/ppermute | solution.py:538
  202.2 1.2 copy-start.37
  203.4 1.2 copy-start.39
  204.7 0.9 copy-start.42
  205.6 1.2 copy-start.44
  209.9 1.0 copy-start.12
  210.9 1.0 copy-start.14
  211.9 1.0 copy-start.16
  212.9 1.6 copy-start.5
  214.5 0.9 copy-start.31
  219.3 60.4 %copy-start.27 = (bf16[512,256]{1,0:T(8,128)(2,1)S(1)}, bf16[512,256]{1,0:T(8,128)(2,1)}, u32[]{:S(2)}) copy-start(bf16[512,256]{1,0:T(8,128)(2,1)} %constant.45.clone.table_high) | copy-start | bytes 786436
  219.3 60.4 %copy-start.34 = (f32[16,2,256]{2,1,0:T(2,128)S(1)}, f32[16,2,256]{2,1,0:T(2,128)}, u32[]{:S(2)}) copy-start(f32[16,2,256]{2,1,0:T(2,128)} %copy-done.32) | copy-start | bytes 98308
  279.6 5.7 %copy-start.13 = (f32[128,2048]{1,0:T(8,128)S(1)}, f32[128,2048]{1,0:T(8,128)}, u32[]{:S(2)}) copy-start(f32[128,2048]{1,0:T(8,128)} %copy-done.12) | copy-start | bytes 3145732
  279.6 5.7 %copy-start.15 = (f32[128,2048]{1,0:T(8,128)S(1)}, f32[128,2048]{1,0:T(8,128)}, u32[]{:S(2)}) copy-start(f32[128,2048]{1,0:T(8,128)} %copy-done.14) | copy-start | bytes 3145732
  279.6 5.7 %copy-start.17 = (f32[1,128,2048]{2,1,0:T(8,128)S(1)}, f32[1,128,2048]{2,1,0:T(8,128)}, u32[]{:S(2)}) copy-start(f32[1,128,2048]{2,1,0:T(8,128)} %copy-done.16) | copy-start | bytes 3145732
  282.7 2.7 collective-permute-start.9
